TPU v7x, 32 devices: a whole 2x2x4 slice. The times are simulated.
32 devices in a mesh: row: 4 (over y, core), col: 4 (over z), dp: 2 (over x).
Axes of the slice: x: 2, y: 2, z: 4, core: 2. Of those that a mesh axis runs over, the one named last changes fastest.
Arguments:
- observed: bfloat16 [1024, 2048], P(('row', 'dp'), 'col'), may hold values from -6 to 6
- next_observed: bfloat16 [1024, 2048], P(('row', 'dp'), 'col'), may hold values from -6 to 6
- actions: bfloat16 [1024, 128], P(('row', 'dp')), may hold values from -1 to 1
- next_mean: bfloat16 [1024, 128], P(('row', 'dp')), may hold values from -1.1953125 to 1.1953125
- policy_noise: float32 [1024, 128], P(('row', 'dp')), may hold values from -1.5 to 1.5
- rewards: bfloat16 [1024], P(('row', 'dp')), may hold values from -5 to 5
- discounts: bfloat16 [1024], P(('row', 'dp')), may hold values from 0.5 to 0.98828125
- actor_flags: int32 [1024], P(('row', 'dp')), may hold values 0 or 1
- critic_in: float32 [2, 2048, 2048], P(None, 'col', 'row'), may hold values from -0.125 to 0.125
- critic_act: float32 [2, 128, 2048], P(None, None, 'col'), may hold values from -0.5 to 0.5
- critic_head: float32 [2, 2048], P(None, 'row'), may hold values from -0.125 to 0.125
- target_in: float32 [2, 2048, 2048], P(None, 'col', 'row'), may hold values from -0.125 to 0.125
- target_act: float32 [2, 128, 2048], P(None, None, 'col'), may hold values from -0.5 to 0.5
- target_head: float32 [2, 2048], P(None, 'row'), may hold values from -0.125 to 0.125
Outputs:
- new_in: float32 [2, 2048, 2048], P(None, 'col', 'row')
- new_act: float32 [2, 128, 2048], P(None, None, 'col')
- new_head: float32 [2, 2048], P(None, 'row')
- new_target_in: float32 [2, 2048, 2048], P(None, 'col', 'row')
- new_target_act: float32 [2, 128, 2048], P(None, None, 'col')
- new_target_head: float32 [2, 2048], P(None, 'row')
- temporal_errors: float32 [2, 1024], P(None, ('row', 'dp'))
- action_slope: float32 [1024, 128], P(('row', 'dp'))
All inputs are finite; a program needn't handle non-finite values. No bound on the sum of `actor_flags` on one device may be relied on, other than what follows from the above.
Results may differ from a plain program's by a relative error of at most 0.008.
Values may be sent and summed in bfloat16 or wider, within the bound.
A program may use at most 128 MiB of HBM per device.

v0:
```python
import functools

import jax
import jax.numpy as jnp
from jax import lax
from jax.experimental import pallas as pl
from jax.experimental.pallas import tpu as pltpu
from jax.sharding import PartitionSpec as P

noise_clip = 0.5
matrix_rate = 0.004
head_rate = 0.0001
blend_rate = 0.005

f32 = jnp.float32
bf16 = jnp.bfloat16
skew = 2


def kernel(dims, observed, next_observed, actions, next_mean, noise, rewards, discounts, flags,
           cin, cact, chead, tin, tact, thead, new_in, new_act, new_head, new_tin, new_tact,
           new_thead, errs_out, push_out, on_own, tg_own, heads, flag_column, columns,
           w16, a16, on_all, tg_all, emb, slopes, delta, rs_out, rs_in, hidden, vals, vt_own, vt_in,
           errs, gh, epad, ga_own, ga_out, ga_in, ga_all, pu_out, pu_in, pz_all,
           on_s, on_r, tg_s, tg_r, fon_s, fon_r, ftg_s, ftg_r, xon_s, xon_r,
           rs_s, rs_r, sl_s, sl_r, xs_s, xs_r, vt_s, vt_r, er_s, er_r, gh_s, gh_r,
           ga_s, ga_r, gb_s, gb_r, pu_s, pu_r, pz_s, pz_r):
    R, C, D, TB, F, H, A = dims
    HI = R // 2
    TC = TB // 2
    row, col, dp = lax.axis_index("row"), lax.axis_index("col"), lax.axis_index("dp")
    hi, lo = row // 2, row % 2
    n = 8 * HI
    m = n // 2

    def copy(src, dst, ssem, rsem, **where):
        return pltpu.make_async_remote_copy(
            src_ref=src, dst_ref=dst, send_sem=ssem, recv_sem=rsem,
            device_id=where, device_id_type=pl.DeviceIdType.MESH)

    on_own[:, :F] = observed[...]
    on_own[:, F:] = actions[...]
    tg_own[:, :F] = next_observed[...]
    tg_own[:, F:F + A] = jnp.clip(
        next_mean[...].astype(f32) + jnp.clip(noise[...], -noise_clip, noise_clip), -1.0, 1.0
    ).astype(bf16)
    epad[...] = jnp.zeros_like(epad)
    epad[4:5, :] = rewards[...].astype(f32)
    epad[5:6, :] = discounts[...].astype(f32)
    tg_own[:, F + A:] = epad[...].T.astype(bf16)
    epad[0:1, :] = flags[...].astype(f32)
    flag_column[...] = epad[...].T[:, 0:1]
    for k in range(2):
        heads[k] = chead[k:k + 1, :]
        heads[2 + k] = thead[k:k + 1, :]

    plane = [(c, d) for d in range(D) for c in range(C) if c or d]
    barrier = pltpu.get_barrier_semaphore()
    for o in range(1, R):
        pl.semaphore_signal(barrier, inc=1, device_id={"row": (row + o) % R},
                            device_id_type=pl.DeviceIdType.MESH)
    for c, d in plane:
        pl.semaphore_signal(barrier, inc=1,
                            device_id={"col": (col + c) % C, "dp": (dp + d) % D},
                            device_id_type=pl.DeviceIdType.MESH)
    pl.semaphore_wait(barrier, R - 1 + len(plane))

    def on_copy(o):
        to = hi * 2 + (1 - lo) if o == 0 else ((hi + o) % HI) * 2 + lo
        return copy(on_own, on_all.at[dp, row], on_s.at[o], on_r.at[o], row=to)

    def tg_copy(o):
        to = hi * 2 + (1 - lo) if o == 0 else ((hi + o) % HI) * 2 + lo
        return copy(tg_own, tg_all.at[row], tg_s.at[o], tg_r.at[o], row=to)

    for o in range(HI):
        on_copy(o).start()
    for o in range(HI):
        tg_copy(o).start()
    on_all[dp, row] = on_own[...]
    tg_all[row] = tg_own[...]
    for k in range(2):
        w16[k] = cin[k].astype(bf16)
        w16[2 + k] = tin[k].astype(bf16)
        a16[k] = cact[k].astype(bf16)
        a16[2 + k] = tact[k].astype(bf16)

    def fon_copy(o, block):
        return copy(on_all.at[dp, block], on_all.at[dp, block], fon_s.at[o], fon_r.at[o],
                    row=hi * 2 + (1 - lo))

    def ftg_copy(o, block):
        return copy(tg_all.at[block], tg_all.at[block], ftg_s.at[o], ftg_r.at[o],
                    row=hi * 2 + (1 - lo))

    def xon_copy(a, o, block, e):
        return copy(on_all.at[dp, block], on_all.at[dp, block], xon_s.at[a, o, e - 1],
                    xon_r.at[a, o, e - 1], dp=(dp + e) % D)

    def rows_of(d, block):
        return pl.ds(pl.multiple_of((d * R + block) * TB, TB), TB)

    def embed_on(d, block):
        x = on_all[d, block]
        for k in range(2):
            mixed = jnp.dot(x[:, F:], a16[k], preferred_element_type=f32)
            emb[k, rows_of(d, block), :] = (x[:, :F].astype(f32) + mixed).astype(bf16)

    def embed_tg(block):
        x = tg_all[block]
        for k in range(2):
            mixed = jnp.dot(x[:, F:F + A], a16[2 + k], preferred_element_type=f32)
            emb[k, rows_of(D, block), :] = (x[:, :F].astype(f32) + mixed).astype(bf16)

    def prepare(a, i):
        block_of = lambda o: ((hi + o) % HI) * 2 + a
        for o in range(HI):
            block = block_of(o)

            @pl.when(i == 4 * o)
            def _():
                @pl.when(lo == a)
                def _():
                    if o > 0:
                        on_copy(o).wait_recv()
                        fon_copy(o, block).start()

                @pl.when(lo != a)
                def _():
                    if o > 0:
                        fon_copy(o, block).wait_recv()
                    else:
                        on_copy(0).wait_recv()
                for e in range(1, D):
                    xon_copy(a, o, block, e).start()
                embed_on(dp, block)

            @pl.when(i == 4 * (HI + o))
            def _():
                @pl.when(lo == a)
                def _():
                    if o > 0:
                        tg_copy(o).wait_recv()
                        ftg_copy(o, block).start()

                @pl.when(lo != a)
                def _():
                    if o > 0:
                        ftg_copy(o, block).wait_recv()
                    else:
                        tg_copy(0).wait_recv()
                embed_tg(block)

    def place(a, i):
        group = i // (4 * HI)
        o = (i // 4) % HI
        kk = (i // 2) % 2
        half = i % 2
        there = (hi + o) % HI
        return group, kk, half, there, there * 2 + a

    def rs_copy(a, i):
        to = (col + 1) % C if a == 0 else (col + C - 1) % C
        return copy(rs_out.at[a, i], rs_in.at[a, i], rs_s.at[a, i], rs_r.at[a, i], col=to)

    def slope_at(d, kk, block, half):
        start = (d * R + block) * TB + half * TC
        return slopes.at[kk, pl.ds(pl.multiple_of(start, TC), TC), :]

    def sl_copy(a, j):
        _, kk, half, there, block = place(a, j)
        at = slope_at(dp, kk, block, half)
        to = (col + C - 1) % C if a == 0 else (col + 1) % C
        return copy(at, at, sl_s.at[a, j], sl_r.at[a, j], col=to)

    def xs_copy(a, j, e):
        _, kk, half, there, block = place(a, j)
        at = slope_at(dp, kk, block, half)
        return copy(at, at, xs_s.at[a, j, e - 1], xs_r.at[a, j, e - 1], dp=(dp + e) % D)

    lane = lax.broadcasted_iota(jnp.int32, (TC, 128), 1)

    def finish(a, i, pre):
        group, kk, half, there, block = place(a, i)
        sigma = jax.nn.sigmoid(pre)
        hid = pre * sigma
        head = heads[group * 2 + kk]
        value = jnp.sum(hid * head, axis=1, keepdims=True)
        at = pl.ds(pl.multiple_of(there * TB + half * TC, TC), TC)
        vals[at, :] += jnp.where(lane == group * 2 + kk, value, 0.0)

        @pl.when(group == 0)
        def _():
            hidden[kk, at, :] = hid.astype(bf16)
            start = (dp * R + block) * TB + half * TC
            slopes[kk, pl.ds(pl.multiple_of(start, TC), TC), :] = (
                head * (sigma * (1.0 + pre * (1.0 - sigma)))).astype(bf16)
            sl_copy(a, i).start()
            for e in range(1, D):
                xs_copy(a, i, e).start()

    vals[...] = jnp.zeros_like(vals)

    def step(s, carry):
        for a in range(2):
            far = col if a == 0 else C - 1 - col
            i = s - skew * far

            @pl.when((i >= 0) & (i < n))
            def _():
                prepare(a, i)
                group, kk, half, there, block = place(a, i)
                start = (jnp.where(group == 0, dp, D) * R + block) * TB + half * TC

                def partial():
                    left = emb[kk, pl.ds(pl.multiple_of(start, TC), TC), :]
                    return jnp.dot(left, w16[group * 2 + kk], preferred_element_type=f32)

                @pl.when(far == 0)
                def _():
                    rs_out[a, i] = partial().astype(bf16)
                    rs_copy(a, i).start()

                @pl.when((far > 0) & (far < C - 1))
                def _():
                    mine = partial()
                    rs_copy(a, i).wait_recv()
                    rs_out[a, i] = (mine + rs_in[a, i].astype(f32)).astype(bf16)
                    rs_copy(a, i).start()

                @pl.when(far == C - 1)
                def _():
                    mine = partial()
                    rs_copy(a, i).wait_recv()
                    finish(a, i, mine + rs_in[a, i].astype(f32))

            j = s - skew * (2 * (C - 1) - far)

            @pl.when((j >= 0) & (j < m) & (far < C - 1))
            def _():
                sl_copy(a, j).wait_recv()

                @pl.when(far > 0)
                def _():
                    sl_copy(a, j).start()
                for e in range(1, D):
                    xs_copy(a, j, e).start()
        return carry

    lax.fori_loop(0, n + skew * (C - 1), step, 0)

    def vt_copy(o):
        return copy(vt_own, vt_in.at[o - 1], vt_s.at[o - 1], vt_r.at[o - 1], row=(row + o) % R)

    def er_copy(x, a):
        c, d = plane[x]
        return copy(errs.at[dp, a], errs.at[dp, a], er_s.at[x], er_r.at[a, x],
                    col=(col + c) % C, dp=(dp + d) % D)

    def gh_copy(x, a):
        c, d = plane[x]
        return copy(gh.at[dp, a], gh.at[dp, a], gh_s.at[x], gh_r.at[a, x],
                    col=(col + c) % C, dp=(dp + d) % D)

    top = lax.broadcasted_iota(jnp.int32, (8, TB), 0)
    for a in range(2):
        @pl.when(col == (C - 1 if a == 0 else 0))
        def _():
            own = []
            for h in range(HI):
                seen = vals[h * TB:(h + 1) * TB, :] + tg_all[h * 2 + a][:, F + A:].astype(f32)
                own.append(seen.T[:8])
                vt_own[h] = own[h]
            for o in range(1, R):
                vt_copy(o).start()
            for o in range(1, R):
                vt_copy(o).wait()
            total = jnp.zeros((8, H), f32)
            for h in range(HI):
                summed = own[h]
                for o in range(1, R):
                    summed = summed + vt_in[o - 1, h]
                goal = own[h][4:5] + own[h][5:6] * jnp.minimum(summed[2:3], summed[3:4])
                err = jnp.where(top < 2, summed - goal, 0.0)
                errs[dp, a, h] = err
                twice = (2.0 * err).astype(bf16)
                for k in range(2):
                    got = jnp.dot(twice, hidden[k, h * TB:(h + 1) * TB, :],
                                  preferred_element_type=f32)
                    keep = lax.broadcasted_iota(jnp.int32, (8, H), 0) == k
                    total = total + jnp.where(keep, got, 0.0)
            for x in range(len(plane)):
                er_copy(x, a).start()
            gh[dp, a] = total
            for x in range(len(plane)):
                gh_copy(x, a).start()

    def late(s, carry):
        for a in range(2):
            far = col if a == 0 else C - 1 - col
            j = s - skew * (2 * (C - 1) - far)

            @pl.when((j >= 0) & (j < m) & (far < C - 1))
            def _():
                sl_copy(a, j).wait_recv()

                @pl.when(far > 0)
                def _():
                    sl_copy(a, j).start()
                for e in range(1, D):
                    xs_copy(a, j, e).start()
        return carry

    lax.fori_loop(n + skew * (C - 1), max(n + skew * (C - 1), m + 2 * skew * (C - 1)), late, 0)

    def pu_copy(o):
        return copy(pu_out.at[o], pu_in.at[o - 1], pu_s.at[o - 1], pu_r.at[o - 1],
                    row=(row + o) % R)

    def pz_copy(c):
        return copy(pz_all.at[col], pz_all.at[col], pz_s.at[c - 1], pz_r.at[c - 1],
                    col=(col + c) % C)

    lift = jnp.dot(a16[0], w16[0], preferred_element_type=f32).astype(bf16)
    last = (((1,), (1,)), ((), ()))
    first = (((0,), (0,)), ((), ()))
    own_push = None
    for o in range(R):
        got = lax.dot_general(slopes[0, rows_of(dp, (row + o) % R), :], lift, last,
                              preferred_element_type=f32)
        if o == 0:
            own_push = got
        else:
            pu_out[o] = got.astype(bf16)
            pu_copy(o).start()

    for e in range(1, D):
        src = (dp + D - e) % D
        for a in range(2):
            for o in range(HI):
                block = ((hi + o) % HI) * 2 + a
                xon_copy(a, o, block, e).wait_recv()
                embed_on(src, block)

    for o in range(1, R):
        pu_copy(o).wait_recv()
        own_push = own_push + pu_in[o - 1].astype(f32)
    pz_all[col] = own_push.astype(bf16)
    for c in range(1, C):
        pz_copy(c).start()

    for e in range(1, D):
        def take(j, carry):
            for a in range(2):
                xs_copy(a, j, e).wait_recv()
            return carry
        lax.fori_loop(0, m, take, 0)

    for a in range(2):
        end = C - 1 if a == 0 else 0
        for x, (c, d) in enumerate(plane):
            @pl.when((col + C - c) % C == end)
            def _():
                er_copy(x, a).wait_recv()

    epad[...] = jnp.zeros_like(epad)
    for d in range(D):
        for h in range(HI):
            for a in range(2):
                epad[0:8, :] = 2.0 * errs[d, a, h]
                at = slice((d * R + h * 2 + a) * TB, (d * R + h * 2 + a + 1) * TB)
                columns[at, :] = epad[...].T

    FR = F // R

    def ga_copy(o):
        to = (row + o) % R
        return copy(ga_out.at[to], ga_in.at[o - 1], ga_s.at[o - 1], ga_r.at[o - 1], row=to)

    def gb_copy(o):
        return copy(ga_all.at[row], ga_all.at[row], gb_s.at[o - 1], gb_r.at[o - 1],
                    row=(row + o) % R)

    for k in range(2):
        moved = jnp.zeros((A, H), f32)
        for d in range(D):
            for b in range(R):
                at = slice((d * R + b) * TB, (d * R + b + 1) * TB)
                scaled = columns[at, k:k + 1] * on_all[d, b][:, F:].astype(f32)
                moved = moved + lax.dot_general(scaled.astype(bf16), slopes[k, at, :], first,
                                                preferred_element_type=f32)
        term = lax.dot_general(moved.astype(bf16), w16[k], last, preferred_element_type=f32)
        for p in range(R):
            piece = term[:, p * FR:(p + 1) * FR]
            ga_own[p, k] = piece
            ga_out[p, k] = piece.astype(bf16)
    for o in range(1, R):
        ga_copy(o).start()

    def blend(fresh, target):
        return blend_rate * fresh + (1.0 - blend_rate) * target

    def grad_in(k):
        for b in range(D * R):
            at = slice(b * TB, (b + 1) * TB)
            scaled = columns[at, k:k + 1] * slopes[k, at, :].astype(f32)
            delta[k, at, :] = scaled.astype(bf16)

        def add(d, carry):
            at = pl.ds(pl.multiple_of(d * R * TB, R * TB), R * TB)
            new_in[k] += lax.dot_general(emb[k, at, :], delta[k, at, :], first,
                                         preferred_element_type=f32)
            return carry
        new_in[k] = lax.dot_general(emb[k, :R * TB, :], delta[k, :R * TB, :], first,
                                    preferred_element_type=f32)
        lax.fori_loop(1, D, add, 0)
        fresh = cin[k] - matrix_rate * new_in[k]
        new_in[k] = fresh
        new_tin[k] = blend(fresh, tin[k])

    grad_in(0)
    for o in range(1, R):
        ga_copy(o).wait_recv()
    for k in range(2):
        piece = ga_own[row, k]
        for o in range(1, R):
            piece = piece + ga_in[o - 1, k].astype(f32)
        ga_all[row, k] = piece.astype(bf16)
    for o in range(1, R):
        gb_copy(o).start()
    grad_in(1)

    for c in range(1, C):
        pz_copy(c).wait_recv()
    push = pz_all[0].astype(f32)
    for c in range(1, C):
        push = push + pz_all[c].astype(f32)
    push_out[...] = push * flag_column[...]
    errs_out[...] = errs[dp, lo, hi, 0:2, :]

    for a in range(2):
        end = C - 1 if a == 0 else 0
        for x, (c, d) in enumerate(plane):
            @pl.when((col + C - c) % C == end)
            def _():
                gh_copy(x, a).wait_recv()
    whole = gh[0, 0]
    for d in range(D):
        for a in range(2):
            if d or a:
                whole = whole + gh[d, a]
    new_head[...] = chead[...] - head_rate * whole[:2]
    new_thead[...] = blend(new_head[...], thead[...])

    for o in range(1, R):
        gb_copy(o).wait_recv()
    for p in range(R):
        for k in range(2):
            part = slice(p * FR, (p + 1) * FR)
            fresh = cact[k, :, part] - matrix_rate * ga_all[p, k].astype(f32)
            new_act[k, :, part] = fresh
            new_tact[k, :, part] = blend(fresh, tact[k, :, part])

    for o in range(HI):
        on_copy(o).wait_send()
        tg_copy(o).wait_send()
        if o > 0:
            fon_copy(o, row).wait_send()
            ftg_copy(o, row).wait_send()
        for a in range(2):
            for e in range(1, D):
                xon_copy(a, o, row, e).wait_send()
    for a in range(2):
        far = col if a == 0 else C - 1 - col

        @pl.when(far < C - 1)
        def _():
            def left(i, carry):
                rs_copy(a, i).wait_send()
                return carry
            lax.fori_loop(0, n, left, 0)

        @pl.when(far > 0)
        def _():
            def left(j, carry):
                sl_copy(a, j).wait_send()
                return carry
            lax.fori_loop(0, m, left, 0)

        def gone(j, carry):
            for e in range(1, D):
                xs_copy(a, j, e).wait_send()
            return carry
        lax.fori_loop(0, m, gone, 0)

        @pl.when(far == C - 1)
        def _():
            for x in range(len(plane)):
                er_copy(x, a).wait_send()
                gh_copy(x, a).wait_send()
    for o in range(1, R):
        pu_copy(o).wait_send()
        ga_copy(o).wait_send()
        gb_copy(o).wait_send()
    for c in range(1, C):
        pz_copy(c).wait_send()


def on_device(dims, observed, next_observed, actions, next_mean, policy_noise, rewards, discounts,
              actor_flags, critic_in, critic_act, critic_head, target_in, target_act, target_head):
    R, C, D, TB, F, H, A = dims
    HI, TC = R // 2, TB // 2
    n, m, planes = 8 * HI, 4 * HI, C * D - 1
    dma = lambda *shape: pltpu.SemaphoreType.DMA(shape)
    vmem = pltpu.VMEM
    scratch = [
        vmem((TB, F + A), bf16), vmem((TB, F + A + 128), bf16), vmem((4, 1, H), f32),
        vmem((TB, 1), f32), vmem((D * R * TB, 128), f32),
        vmem((4, F, H), bf16), vmem((4, A, F), bf16),
        vmem((D, R, TB, F + A), bf16), vmem((R, TB, F + A + 128), bf16),
        vmem((2, (D + 1) * R * TB, F), bf16),
        vmem((2, D * R * TB, H), bf16), vmem((2, D * R * TB, H), bf16),
        vmem((2, n, TC, H), bf16), vmem((2, n, TC, H), bf16),
        vmem((2, HI * TB, H), bf16), vmem((HI * TB, 128), f32),
        vmem((HI, 8, TB), f32), vmem((R - 1, HI, 8, TB), f32),
        vmem((D, 2, HI, 8, TB), f32), vmem((D, 2, 8, H), f32), vmem((128, TB), f32),
        vmem((R, 2, A, F // R), f32), vmem((R, 2, A, F // R), bf16),
        vmem((R - 1, 2, A, F // R), bf16), vmem((R, 2, A, F // R), bf16),
        vmem((R, TB, A), bf16), vmem((R - 1, TB, A), bf16), vmem((C, TB, A), bf16),
        dma(HI), dma(HI), dma(HI), dma(HI),
        dma(HI), dma(HI), dma(HI), dma(HI),
        dma(2, HI, D - 1), dma(2, HI, D - 1),
        dma(2, n), dma(2, n), dma(2, m), dma(2, m),
        dma(2, m, D - 1), dma(2, m, D - 1),
        dma(R - 1), dma(R - 1),
        dma(planes), dma(2, planes), dma(planes), dma(2, planes),
        dma(R - 1), dma(R - 1), dma(R - 1), dma(R - 1),
        dma(R - 1), dma(R - 1), dma(C - 1), dma(C - 1),
    ]
    spec = pl.BlockSpec(memory_space=vmem)
    shaped = jax.ShapeDtypeStruct
    return pl.pallas_call(
        functools.partial(kernel, dims),
        out_shape=(shaped((2, F, H), f32), shaped((2, A, F), f32), shaped((2, H), f32),
                   shaped((2, F, H), f32), shaped((2, A, F), f32), shaped((2, H), f32),
                   shaped((2, TB), f32), shaped((TB, A), f32)),
        in_specs=[spec] * 14,
        out_specs=(spec,) * 8,
        scratch_shapes=scratch,
        compiler_params=pltpu.CompilerParams(
            collective_id=0, has_side_effects=True, vmem_limit_bytes=67043328),
    )(observed, next_observed, actions, next_mean, policy_noise, rewards[None, :],
      discounts[None, :], actor_flags[None, :], critic_in, critic_act, critic_head, target_in,
      target_act, target_head)


def solution(mesh):
    def run(*args):
        R, C, D = mesh.shape["row"], mesh.shape["col"], mesh.shape["dp"]
        tokens, features = args[0].shape
        dims = (R, C, D, tokens // (R * D), features // C, args[8].shape[2] // R,
                args[2].shape[1])
        return sharded(dims)(*args)

    def sharded(dims):
        return jax.shard_map(
            functools.partial(on_device, dims),
            mesh=mesh,
            in_specs=(
                P(("row", "dp"), "col"),
                P(("row", "dp"), "col"),
                P(("row", "dp"), None),
                P(("row", "dp"), None),
                P(("row", "dp"), None),
                P(("row", "dp")),
                P(("row", "dp")),
                P(("row", "dp")),
                P(None, "col", "row"),
                P(None, None, "col"),
                P(None, "row"),
                P(None, "col", "row"),
                P(None, None, "col"),
                P(None, "row"),
            ),
            out_specs=(
                P(None, "col", "row"),
                P(None, None, "col"),
                P(None, "row"),
                P(None, "col", "row"),
                P(None, None, "col"),
                P(None, "row"),
                P(None, ("row", "dp")),
                P(("row", "dp"), None),
            ),
            check_vma=False,
        )

    return run
```

profile of v0, /device:TPU:0, one launch (start us, length us, event | category | flops | bytes accessed | tf_op | source)
XLA Modules:
  0.0 88.7 jit_solution(7763442560759126825)
XLA Ops:
  0.6 79.5 %shard_map.197 = (f32[2,512,512]{2,1,0:T(8,128)}, f32[2,128,512]{2,1,0:T(8,128)}, f32[2,512]{1,0:T(2,128)}, f32[2,512,512]{2,1,0:T(8,128)}, f32[2,128,512]{2,1,0...) custom-call(bf16[128,512]{1,0:T(8,128)(2,1)} %observed.1, bf16[128,512]{1,0:T(8,128)(2,1)} %next_observed.1, ...), custom_call_target="tpu_custom_call" | custom-call | tf_op jit(solution)/shard_map/pallas_call | solution.py:542
  80.2 0.0 copy-start.2
  80.2 0.0 copy-start.5
  80.2 0.0 copy-start
  80.2 3.2 %copy.30 = f32[2,512,512]{2,1,0:T(8,128)} copy(f32[2,512,512]{2,1,0:T(8,128)} %get-tuple-element.16) | data formatting | bytes 4194304
  83.4 0.0 copy-done.2
  83.4 0.8 copy.31
  84.2 0.0 copy-done.5
  84.2 0.6 copy.32
  84.8 0.0 copy-done
  84.8 0.0 copy-start.1
  84.8 0.0 copy-start.4
  84.8 0.0 copy-start.6
  84.8 0.0 copy-start.3
  84.8 1.3 %copy.33 = f32[2,512,512]{2,1,0:T(8,128)} copy(f32[2,512,512]{2,1,0:T(8,128)S(1)} %copy-done) | data formatting | bytes 4194304
  86.2 0.0 copy-done.1
  86.2 0.8 copy.34
  87.0 0.0 copy-done.4
  87.0 0.6 copy.35
  87.5 0.0 copy-done.6
  87.6 0.6 copy.36
  88.1 0.0 copy-done.3
  88.1 0.6 copy.37
Async XLA Ops:
  80.2 3.3 %copy-start.2 = (f32[2,128,512]{2,1,0:T(8,128)S(1)}, f32[2,128,512]{2,1,0:T(8,128)}, u32[]{:S(2)}) copy-start(f32[2,128,512]{2,1,0:T(8,128)} %get-tuple-element.17) | copy-start | bytes 1572868
  80.2 4.0 %copy-start.5 = (f32[2,512]{1,0:T(2,128)S(1)}, f32[2,512]{1,0:T(2,128)}, u32[]{:S(2)}) copy-start(f32[2,512]{1,0:T(2,128)} %get-tuple-element.18) | copy-start | bytes 12292
  80.2 4.6 %copy-start = (f32[2,512,512]{2,1,0:T(8,128)S(1)}, f32[2,512,512]{2,1,0:T(8,128)}, u32[]{:S(2)}) copy-start(f32[2,512,512]{2,1,0:T(8,128)} %get-tuple-element.19) | copy-start | bytes 6291460
  84.8 1.4 %copy-start.1 = (f32[2,128,512]{2,1,0:T(8,128)S(1)}, f32[2,128,512]{2,1,0:T(8,128)}, u32[]{:S(2)}) copy-start(f32[2,128,512]{2,1,0:T(8,128)} %get-tuple-element.20) | copy-start | bytes 1572868
  84.8 2.1 %copy-start.4 = (f32[2,512]{1,0:T(2,128)S(1)}, f32[2,512]{1,0:T(2,128)}, u32[]{:S(2)}) copy-start(f32[2,512]{1,0:T(2,128)} %get-tuple-element.21) | copy-start | bytes 12292
  84.8 2.7 %copy-start.6 = (f32[2,128]{1,0:T(2,128)S(1)}, f32[2,128]{1,0:T(2,128)}, u32[]{:S(2)}) copy-start(f32[2,128]{1,0:T(2,128)} %get-tuple-element.22) | copy-start | bytes 3076
  84.8 3.3 %copy-start.3 = (f32[128,128]{1,0:T(8,128)S(1)}, f32[128,128]{1,0:T(8,128)}, u32[]{:S(2)}) copy-start(f32[128,128]{1,0:T(8,128)} %get-tuple-element.23) | copy-start | bytes 196612
where the time goes:
time: 89.5 us; the launch traced here: 88.7 us
  Pallas kernels  79.5 us (89%)
  local copies, waits for them, and re-layouts  8.55 us (10%)
    pallas_call x1, Pallas kernels, on_device(): pl.pallas_call(functools.partial(kernel, dims), out_shape=(shaped((2, F,...  79.5 us
    unnamed x22, local copies, waits for them, and re-layouts  8.55 us

commit v1 on v0

--- a/solution.py
+++ b/solution.py
@@ -17,14 +17,15 @@
 skew = 2
 
 
-def kernel(dims, observed, next_observed, actions, next_mean, noise, rewards, discounts, flags,
-           cin, cact, chead, tin, tact, thead, new_in, new_act, new_head, new_tin, new_tact,
+def kernel(dims, observed_at, next_observed_at, actions_at, next_mean_at, noise_at, rewards_at,
+           discounts_at, flags_at, cin_at, cact_at, chead_at, tin_at, tact_at, thead_at, new_in, new_act, new_head, new_tin, new_tact,
            new_thead, errs_out, push_out, on_own, tg_own, heads, flag_column, columns,
            w16, a16, on_all, tg_all, emb, slopes, delta, rs_out, rs_in, hidden, vals, vt_own, vt_in,
            errs, gh, epad, ga_own, ga_out, ga_in, ga_all, pu_out, pu_in, pz_all,
            on_s, on_r, tg_s, tg_r, fon_s, fon_r, ftg_s, ftg_r, xon_s, xon_r,
            rs_s, rs_r, sl_s, sl_r, xs_s, xs_r, vt_s, vt_r, er_s, er_r, gh_s, gh_r,
-           ga_s, ga_r, gb_s, gb_r, pu_s, pu_r, pz_s, pz_r):
+           ga_s, ga_r, gb_s, gb_r, pu_s, pu_r, pz_s, pz_r, next_mean, noise, rewards, discounts,
+           flags, cin, cact, chead, tin, tact, thead, load_s):
     R, C, D, TB, F, H, A = dims
     HI = R // 2
     TC = TB // 2
@@ -38,21 +39,15 @@
             src_ref=src, dst_ref=dst, send_sem=ssem, recv_sem=rsem,
             device_id=where, device_id_type=pl.DeviceIdType.MESH)
 
-    on_own[:, :F] = observed[...]
-    on_own[:, F:] = actions[...]
-    tg_own[:, :F] = next_observed[...]
-    tg_own[:, F:F + A] = jnp.clip(
-        next_mean[...].astype(f32) + jnp.clip(noise[...], -noise_clip, noise_clip), -1.0, 1.0
-    ).astype(bf16)
-    epad[...] = jnp.zeros_like(epad)
-    epad[4:5, :] = rewards[...].astype(f32)
-    epad[5:6, :] = discounts[...].astype(f32)
-    tg_own[:, F + A:] = epad[...].T.astype(bf16)
-    epad[0:1, :] = flags[...].astype(f32)
-    flag_column[...] = epad[...].T[:, 0:1]
-    for k in range(2):
-        heads[k] = chead[k:k + 1, :]
-        heads[2 + k] = thead[k:k + 1, :]
+    pairs = [(observed_at, on_own.at[:, :F]), (actions_at, on_own.at[:, F:]),
+             (next_observed_at, tg_own.at[:, :F]), (next_mean_at, next_mean), (noise_at, noise),
+             (rewards_at, rewards), (discounts_at, discounts), (flags_at, flags),
+             (cact_at, cact), (cin_at.at[0], cin.at[0]), (cin_at.at[1], cin.at[1]),
+             (tact_at, tact), (tin_at.at[0], tin.at[0]), (tin_at.at[1], tin.at[1]),
+             (chead_at, chead), (thead_at, thead)]
+    loads = [pltpu.make_async_copy(src, dst, load_s.at[x]) for x, (src, dst) in enumerate(pairs)]
+    for load in loads:
+        load.start()
 
     plane = [(c, d) for d in range(D) for c in range(C) if c or d]
     barrier = pltpu.get_barrier_semaphore()
@@ -73,12 +68,30 @@
         to = hi * 2 + (1 - lo) if o == 0 else ((hi + o) % HI) * 2 + lo
         return copy(tg_own, tg_all.at[row], tg_s.at[o], tg_r.at[o], row=to)
 
+    for x in range(2):
+        loads[x].wait()
     for o in range(HI):
         on_copy(o).start()
+    for x in range(2, 8):
+        loads[x].wait()
+    tg_own[:, F:F + A] = jnp.clip(
+        next_mean[...].astype(f32) + jnp.clip(noise[...], -noise_clip, noise_clip), -1.0, 1.0
+    ).astype(bf16)
+    epad[...] = jnp.zeros_like(epad)
+    epad[4:5, :] = rewards[...].astype(f32)
+    epad[5:6, :] = discounts[...].astype(f32)
+    tg_own[:, F + A:] = epad[...].T.astype(bf16)
+    epad[0:1, :] = flags[...].astype(f32)
+    flag_column[...] = epad[...].T[:, 0:1]
     for o in range(HI):
         tg_copy(o).start()
     on_all[dp, row] = on_own[...]
     tg_all[row] = tg_own[...]
+    for x in range(8, 16):
+        loads[x].wait()
+    for k in range(2):
+        heads[k] = chead[k:k + 1, :]
+        heads[2 + k] = thead[k:k + 1, :]
     for k in range(2):
         w16[k] = cin[k].astype(bf16)
         w16[2 + k] = tin[k].astype(bf16)
@@ -536,22 +549,42 @@
         dma(planes), dma(2, planes), dma(planes), dma(2, planes),
         dma(R - 1), dma(R - 1), dma(R - 1), dma(R - 1),
         dma(R - 1), dma(R - 1), dma(C - 1), dma(C - 1),
+        vmem((TB, A), bf16), vmem((TB, A), f32), vmem((1, TB), bf16), vmem((1, TB), bf16),
+        vmem((1, TB), jnp.int32), vmem((2, F, H), f32), vmem((2, A, F), f32), vmem((2, H), f32),
+        vmem((2, F, H), f32), vmem((2, A, F), f32), vmem((2, H), f32), dma(16),
     ]
     spec = pl.BlockSpec(memory_space=vmem)
-    shaped = jax.ShapeDtypeStruct
-    return pl.pallas_call(
+    results = (((2, F, H), f32), ((2, A, F), f32), ((2, H), f32), ((2, F, H), f32),
+               ((2, A, F), f32), ((2, H), f32), ((2, TB), f32), ((TB, A), f32))
+    kept = pl.pallas_call(
         functools.partial(kernel, dims),
-        out_shape=(shaped((2, F, H), f32), shaped((2, A, F), f32), shaped((2, H), f32),
-                   shaped((2, F, H), f32), shaped((2, A, F), f32), shaped((2, H), f32),
-                   shaped((2, TB), f32), shaped((TB, A), f32)),
-        in_specs=[spec] * 14,
+        out_shape=tuple(vmem(shape, kind) for shape, kind in results),
+        in_specs=[pl.BlockSpec(memory_space=pltpu.HBM)] * 14,
         out_specs=(spec,) * 8,
         scratch_shapes=scratch,
         compiler_params=pltpu.CompilerParams(
-            collective_id=0, has_side_effects=True, vmem_limit_bytes=67043328),
-    )(observed, next_observed, actions, next_mean, policy_noise, rewards[None, :],
-      discounts[None, :], actor_flags[None, :], critic_in, critic_act, critic_head, target_in,
-      target_act, target_head)
+            collective_id=0, has_side_effects=True, vmem_limit_bytes=57 * 2 ** 20),
+    )(*[pltpu.with_memory_space_constraint(one, pltpu.HBM) for one in (
+        observed, next_observed, actions, next_mean, policy_noise, rewards[None, :],
+        discounts[None, :], actor_flags[None, :], critic_in, critic_act, critic_head, target_in,
+        target_act, target_head)])
+    return pl.pallas_call(
+        put_out,
+        out_shape=tuple(jax.ShapeDtypeStruct(shape, kind) for shape, kind in results),
+        in_specs=[spec] * 8,
+        out_specs=(pl.BlockSpec(memory_space=pl.ANY),) * 8,
+        scratch_shapes=[dma(8)],
+        compiler_params=pltpu.CompilerParams(vmem_limit_bytes=12 * 2 ** 20),
+    )(*[pltpu.with_memory_space_constraint(one, vmem) for one in kept])
+
+
+def put_out(*refs):
+    sems = refs[16]
+    copies = [pltpu.make_async_copy(refs[x], refs[8 + x], sems.at[x]) for x in range(8)]
+    for one in copies:
+        one.start()
+    for one in copies:
+        one.wait()
 
 
 def solution(mesh):

time: 89.5 us -> 78.6 us (0.88)
  local copies, waits for them, and re-layouts: 8.55 us -> 0 us
  Pallas kernels: 79.5 us -> 77.2 us
    unnamed x22 -> x0, local copies, waits for them, and re-layouts: 8.55 us -> none
    pallas_call x1 -> x2, Pallas kernels: 79.5 us -> 77.2 us  [the longest x1 74.8 us: on_device(): pl.pallas_call(functools.partial(kernel, dims), out_shape=tuple((vmem(sha...]
where the time goes in v1:
time: 78.6 us; the launch traced here: 77.9 us
  Pallas kernels  77.2 us (98%)
    pallas_call x1, Pallas kernels, on_device(): pl.pallas_call(functools.partial(kernel, dims), out_shape=tuple((vmem(sha...  74.8 us
    pallas_call x1, Pallas kernels, on_device(): pl.pallas_call(put_out, out_shape=tuple((jax.ShapeDtypeStruct(shape, kind...  2.43 us

profile of v1, /device:TPU:0, one launch (start us, length us, event | category | flops | bytes accessed | tf_op | source)
XLA Modules:
  0.0 77.9 jit_solution(16076717632058319927)
XLA Ops:
  0.6 74.8 %shard_map.197 = (f32[2,512,512]{2,1,0:T(8,128)S(1)}, f32[2,128,512]{2,1,0:T(8,128)S(1)}, f32[2,512]{1,0:T(2,128)S(1)}, f32[2,512,512]{2,1,0:T(8,128)S(1)}, f32[...) custom-call(bf16[128,512]{1,0:T(8,128)(2,1)} %observed_at.1, ...), custom_call_target="tpu_custom_call" | custom-call | tf_op jit(solution)/shard_map/pallas_call | solution.py:559
  75.4 2.4 %shard_map.198 = (f32[2,512,512]{2,1,0:T(8,128)}, f32[2,128,512]{2,1,0:T(8,128)}, f32[2,512]{1,0:T(2,128)}, f32[2,512,512]{2,1,0:T(8,128)}, f32[2,128,512]{2,1,0...) custom-call(f32[2,512,512]{2,1,0:T(8,128)S(1)} %get-tuple-element.16.refs_0_, ...), custom_call_target="tpu_custom_call" | custom-call | tf_op jit(solution)/shard_map/pallas_call | solution.py:571

commit v2 on v1

v2 whole, which is shorter than its diff:
```python
import functools

import jax
import jax.numpy as jnp
from jax import lax
from jax.experimental import pallas as pl
from jax.experimental.pallas import tpu as pltpu
from jax.sharding import PartitionSpec as P

noise_clip = 0.5
matrix_rate = 0.004
head_rate = 0.0001
blend_rate = 0.005

f32 = jnp.float32
bf16 = jnp.bfloat16
skew = 3
pieces = 2


def kernel(dims, observed_at, next_observed_at, actions_at, next_mean_at, noise_at, rewards_at,
           discounts_at, flags_at, cin_at, cact_at, chead_at, tin_at, tact_at, thead_at,
           new_in, new_act, new_head, new_tin, new_tact, new_thead, errs_out, push_out,
           next_mean, noise, rewards, discounts, flags, cin, cact, chead, tin, tact, thead,
           on_own, tg_own, flag_column, w16, a16, on_all, tg_all, emb, slopes, delta, lift,
           t_out, t_in, o_out, o_in, hidden, vals_t, vals_o, rd_own, rd_all, vt_all, vo_all, gl,
           err_own, err_top, gh, epad, columns, scaled,
           ga_own, ga_out, ga_in, gb_all, gc_all, pu_out, pu_in, pz_all,
           load_s, on_s, on_r, tg_s, tg_r, ftg_s, ftg_r, ox_s, ox_r, oo_s, oo_r, rd_s, rd_r,
           tr_s, tr_r, or_s, or_r, xs_s, xs_r, vt_s, vt_r, vo_s, vo_r, gl_s, gl_r, er_s, er_r,
           gh_s, gh_r, ga_s, ga_r, gb_s, gb_r, gc_s, gc_r, pu_s, pu_r, pz_s, pz_r):
    R, C, D, TB, F, H, A = dims
    HI = R // 2
    TC = TB // pieces
    row, col, dp = lax.axis_index("row"), lax.axis_index("col"), lax.axis_index("dp")
    hi, lo = row // 2, row % 2
    nt = 2 * HI * pieces
    no = 2 * R * pieces
    partner = hi * 2 + (1 - lo)

    def copy(src, dst, ssem, rsem, **where):
        return pltpu.make_async_remote_copy(
            src_ref=src, dst_ref=dst, send_sem=ssem, recv_sem=rsem,
            device_id=where, device_id_type=pl.DeviceIdType.MESH)

    pairs = [(next_observed_at, tg_own.at[:, :F]), (next_mean_at, next_mean), (noise_at, noise),
             (tact_at, tact), (tin_at.at[0], tin.at[0]), (tin_at.at[1], tin.at[1]),
             (thead_at, thead), (observed_at, on_own.at[:, :F]), (actions_at, on_own.at[:, F:]),
             (rewards_at, rewards), (discounts_at, discounts), (flags_at, flags),
             (cact_at, cact), (cin_at.at[0], cin.at[0]), (cin_at.at[1], cin.at[1]),
             (chead_at, chead)]
    loads = [pltpu.make_async_copy(src, dst, load_s.at[x]) for x, (src, dst) in enumerate(pairs)]
    for load in loads:
        load.start()

    plane = [(c, d) for d in range(D) for c in range(C) if c or d]
    group = [(r, d) for d in range(D) for r in range(R) if r or d]
    others = [(r, 0, d) for r, d in group] + [(0, c, d) for c, d in plane if c]
    barrier = pltpu.get_barrier_semaphore()
    for r, c, d in others:
        pl.semaphore_signal(barrier, inc=1,
                            device_id={"row": (row + r) % R, "col": (col + c) % C,
                                       "dp": (dp + d) % D},
                            device_id_type=pl.DeviceIdType.MESH)

    vals_t[...] = jnp.zeros_like(vals_t)
    vals_o[...] = jnp.zeros_like(vals_o)
    for x in range(3):
        loads[x].wait()
    tg_own[:, F:] = jnp.clip(
        next_mean[...].astype(f32) + jnp.clip(noise[...], -noise_clip, noise_clip), -1.0, 1.0
    ).astype(bf16)
    pl.semaphore_wait(barrier, len(others))

    def tg_copy(o):
        to = partner if o == 0 else ((hi + o) % HI) * 2 + lo
        return copy(tg_own, tg_all.at[row], tg_s.at[o], tg_r.at[o], row=to)

    def ftg_copy(o, block):
        return copy(tg_all.at[block], tg_all.at[block], ftg_s.at[o], ftg_r.at[o], row=partner)

    def on_copy(o):
        return copy(on_own, on_all.at[dp, row], on_s.at[o - 1], on_r.at[o - 1],
                    row=(row + o) % R)

    def ox_copy(e):
        return copy(on_own, on_all.at[dp, row], ox_s.at[e - 1], ox_r.at[e - 1], dp=(dp + e) % D)

    def oo_copy(e, o):
        at = on_all.at[(dp + D - e) % D, row]
        return copy(at, at, oo_s.at[e - 1, o - 1], oo_r.at[e - 1, o - 1], row=(row + o) % R)

    def rd_copy(o):
        return copy(rd_own, rd_all.at[row], rd_s.at[o - 1], rd_r.at[o - 1], row=(row + o) % R)

    for o in range(HI):
        tg_copy(o).start()
    tg_all[row] = tg_own[...]
    for x in range(3, 7):
        loads[x].wait()
    for k in range(2):
        a16[2 + k] = tact[k].astype(bf16)
        w16[2 + k] = tin[k].astype(bf16)
    for x in range(7, 12):
        loads[x].wait()
    for e in range(1, D):
        ox_copy(e).start()
    rd_own[...] = jnp.zeros_like(rd_own)
    rd_own[0:1, :] = rewards[...].astype(f32)
    rd_own[1:2, :] = discounts[...].astype(f32)
    for o in range(1, R):
        on_copy(o).start()
        rd_copy(o).start()
    on_all[dp, row] = on_own[...]
    rd_all[row] = rd_own[...]

    def rows_of(d, block):
        return pl.ds(pl.multiple_of((d * R + block) * TB, TB), TB)

    def embed_on(d, block):
        x = on_all[d, block]
        for k in range(2):
            mixed = jnp.dot(x[:, F:], a16[k], preferred_element_type=f32)
            emb[k, rows_of(d, block), :] = (x[:, :F].astype(f32) + mixed).astype(bf16)

    def embed_tg(block):
        x = tg_all[block]
        for k in range(2):
            mixed = jnp.dot(x[:, F:], a16[2 + k], preferred_element_type=f32)
            emb[k, rows_of(D, block), :] = (x[:, :F].astype(f32) + mixed).astype(bf16)

    def prepare_tg(a, i):
        for o in range(HI):
            block = ((hi + HI - o) % HI) * 2 + a

            @pl.when(i == 2 * pieces * o)
            def _():
                @pl.when(lo == a)
                def _():
                    if o > 0:
                        tg_copy(o).wait_recv()
                        ftg_copy(o, block).start()

                @pl.when(lo != a)
                def _():
                    if o > 0:
                        ftg_copy(o, block).wait_recv()
                    else:
                        tg_copy(0).wait_recv()
                embed_tg(block)

    def prepare_on(q):
        for o in range(R):
            @pl.when(q == 2 * pieces * o)
            def _():
                if o > 0:
                    on_copy(o).wait_recv()
                embed_on(dp, (row + R - o) % R)

    def along(a):
        return (col + 1) % C if a == 0 else (col + C - 1) % C

    def tr_copy(a, i):
        return copy(t_out.at[a, i], t_in.at[a, i], tr_s.at[a, i], tr_r.at[a, i], col=along(a))

    def or_copy(a, q):
        return copy(o_out.at[a, q], o_in.at[a, q], or_s.at[a, q], or_r.at[a, q], col=along(a))

    def place_t(a, i):
        block = ((hi + HI - i // (2 * pieces)) % HI) * 2 + a
        return block, (i // pieces) % 2, i % pieces

    def place_o(q):
        return (row + R - q // (2 * pieces)) % R, (q // pieces) % 2, q % pieces

    def chunk(d, block, piece):
        return pl.ds(pl.multiple_of((d * R + block) * TB + piece * TC, TC), TC)

    def xs_copy(q, e):
        block, kk, piece = place_o(q)
        at = slopes.at[kk, chunk(dp, block, piece), :]
        return copy(at, at, xs_s.at[q, e - 1], xs_r.at[q, e - 1], dp=(dp + e) % D)

    def vt_copy(o):
        return copy(vt_all.at[row], vt_all.at[row], vt_s.at[o - 1], vt_r.at[o - 1],
                    row=(row + o) % R)

    def gl_copy(x, a):
        c, d = plane[x]
        return copy(gl.at[dp, a], gl.at[dp, a], gl_s.at[x], gl_r.at[a, x],
                    col=(col + c) % C, dp=(dp + d) % D)

    def vo_copy(x):
        r, d = group[x]
        return copy(vo_all.at[dp, row], vo_all.at[dp, row], vo_s.at[x], vo_r.at[x],
                    row=(row + r) % R, dp=(dp + d) % D)

    lane = lax.broadcasted_iota(jnp.int32, (TC, 128), 1)

    def note(store, block, kk, piece, gate, head):
        value = jnp.sum(gate * head, axis=1, keepdims=True)
        at = pl.ds(pl.multiple_of(piece * TC, TC), TC)
        store[at, :] += jnp.where(lane == kk * R + block, value, 0.0)

    def finish_t(a, i, pre):
        block, kk, piece = place_t(a, i)
        note(vals_t, block, kk, piece, pre * jax.nn.sigmoid(pre), thead[pl.ds(kk, 1), :])

    def finish_o(q, pre):
        block, kk, piece = place_o(q)
        sigma = jax.nn.sigmoid(pre)
        gate = pre * sigma
        head = chead[pl.ds(kk, 1), :]
        slopes[kk, chunk(dp, block, piece), :] = (
            head * (sigma * (1.0 + pre * (1.0 - sigma)))).astype(bf16)
        for e in range(1, D):
            xs_copy(q, e).start()
        hidden[kk, chunk(0, block, piece), :] = gate.astype(bf16)
        note(vals_o, block, kk, piece, gate, head)

    def settle(a, i):
        @pl.when(i == nt)
        def _():
            vt_all[row] = vals_t[...].T[:2 * R]
            for o in range(1, R):
                vt_copy(o).start()

        @pl.when(i == nt + 3)
        def _():
            for o in range(1, R):
                vt_copy(o).wait_recv()
            total = vt_all[0]
            for r in range(1, R):
                total = total + vt_all[r]
            reward = jnp.concatenate([rd_all[b, 0:1] for b in range(R)], axis=0)
            discount = jnp.concatenate([rd_all[b, 1:2] for b in range(R)], axis=0)
            goal = reward + discount * jnp.minimum(total[:R], total[R:])
            mine = lax.broadcasted_iota(jnp.int32, (R, TB), 0) % 2 == a
            goal = jnp.where(mine, goal, 0.0)
            gl[dp, a] = jnp.concatenate([goal, goal], axis=0)
            for x in range(len(plane)):
                gl_copy(x, a).start()

    steps = nt + no + skew * (C - 1)

    def aside(s):
        @pl.when(s == 1)
        def _():
            for x in range(12, 16):
                loads[x].wait()
            for k in range(2):
                a16[k] = cact[k].astype(bf16)
                w16[k] = cin[k].astype(bf16)

        @pl.when(s == 4)
        def _():
            for o in range(1, R):
                rd_copy(o).wait_recv()

        @pl.when(s == nt)
        def _():
            for e in range(1, D):
                ox_copy(e).wait_recv()
                for o in range(1, R):
                    oo_copy(e, o).start()

        @pl.when(s == nt + 1)
        def _():
            lift[...] = jnp.dot(a16[0], w16[0], preferred_element_type=f32).astype(bf16)

        for e in range(1, D):
            for o in range(R):
                @pl.when(s == nt + no // 2 + (e - 1) * R + o)
                def _():
                    if o > 0:
                        oo_copy(e, o).wait_recv()
                    embed_on((dp + D - e) % D, (row + R - o) % R)

    def step(s, carry):
        for a in range(2):
            far = col if a == 0 else C - 1 - col
            i = s - skew * far

            @pl.when((i >= 0) & (i < nt))
            def _():
                prepare_tg(a, i)
                block, kk, piece = place_t(a, i)

                def partial():
                    return jnp.dot(emb[kk, chunk(D, block, piece), :], w16[2 + kk],
                                   preferred_element_type=f32)

                @pl.when(far == 0)
                def _():
                    t_out[a, i] = partial().astype(bf16)
                    tr_copy(a, i).start()

                @pl.when((far > 0) & (far < C - 1))
                def _():
                    mine = partial()
                    tr_copy(a, i).wait_recv()
                    t_out[a, i] = (mine + t_in[a, i].astype(f32)).astype(bf16)
                    tr_copy(a, i).start()

                @pl.when(far == C - 1)
                def _():
                    mine = partial()
                    tr_copy(a, i).wait_recv()
                    finish_t(a, i, mine + t_in[a, i].astype(f32))

            @pl.when((i >= nt) & (i < nt + no))
            def _():
                q = i - nt
                block, kk, piece = place_o(q)
                later = 2 * far > C - 1 if a == 0 else 2 * far >= C - 1

                @pl.when(jnp.logical_not(later))
                def _():
                    prepare_on(q)

                def partial():
                    return jnp.dot(emb[kk, chunk(dp, block, piece), :], w16[kk],
                                   preferred_element_type=f32)

                @pl.when(far == 0)
                def _():
                    o_out[a, q] = partial().astype(bf16)
                    or_copy(a, q).start()

                @pl.when((far > 0) & (far < C - 1))
                def _():
                    mine = partial()
                    or_copy(a, q).wait_recv()
                    mine = mine + o_in[a, q].astype(f32)
                    o_out[a, q] = mine.astype(bf16)
                    or_copy(a, q).start()

                    @pl.when(later)
                    def _():
                        finish_o(q, mine + o_in[1 - a, q].astype(f32))

                @pl.when(far == C - 1)
                def _():
                    mine = partial()
                    or_copy(a, q).wait_recv()
                    finish_o(q, mine + o_in[a, q].astype(f32))

            @pl.when(far == C - 1)
            def _():
                settle(a, i)
        aside(s)
        return carry

    lax.fori_loop(0, steps, step, 0)

    vo_all[dp, row] = vals_o[...].T[:2 * R]
    for x in range(len(group)):
        vo_copy(x).start()

    def pu_copy(o):
        return copy(pu_out.at[o - 1], pu_in.at[o - 1], pu_s.at[o - 1], pu_r.at[o - 1],
                    row=(row + o) % R)

    def pz_copy(c):
        return copy(pz_all.at[col], pz_all.at[col], pz_s.at[c - 1], pz_r.at[c - 1],
                    col=(col + c) % C)

    last = (((1,), (1,)), ((), ()))
    first = (((0,), (0,)), ((), ()))
    own_push = None
    for o in list(range(1, R)) + [0]:
        got = lax.dot_general(slopes[0, rows_of(dp, (row + o) % R), :], lift[...], last,
                              preferred_element_type=f32)
        if o == 0:
            own_push = got
        else:
            pu_out[o - 1] = got.astype(bf16)
            pu_copy(o).start()

    for a in range(2):
        end = C - 1 if a == 0 else 0
        for x, (c, d) in enumerate(plane):
            @pl.when((col + C - c) % C == end)
            def _():
                gl_copy(x, a).wait_recv()

    for o in range(1, R):
        pu_copy(o).wait_recv()
        own_push = own_push + pu_in[o - 1].astype(f32)
    pz_all[col] = own_push.astype(bf16)
    for c in range(1, C):
        pz_copy(c).start()

    for e in range(1, D):
        def take(q, carry):
            xs_copy(q, e).wait_recv()
            return carry
        lax.fori_loop(0, no, take, 0)
    for x in range(len(group)):
        vo_copy(x).wait_recv()

    epad[...] = jnp.zeros_like(epad)
    for d in range(D):
        value = vo_all[d, 0]
        for r in range(1, R):
            value = value + vo_all[d, r]
        err = value - (gl[d, 0] + gl[d, 1])
        err_own[d] = err
        epad[:2 * R, :] = 2.0 * err
        columns[d] = epad[...].T

    F2 = F // 2

    def ga_copy(k):
        return copy(ga_out.at[k], ga_in.at[k], ga_s.at[k], ga_r.at[k], row=partner)

    def gb_copy(k, o):
        return copy(gb_all.at[k, hi], gb_all.at[k, hi], gb_s.at[k, o - 1], gb_r.at[k, o - 1],
                    row=((hi + o) % HI) * 2 + lo)

    def gc_copy(k):
        return copy(gc_all.at[k, lo], gc_all.at[k, lo], gc_s.at[k], gc_r.at[k], row=partner)

    for k in range(2):
        moved = jnp.zeros((A, H), f32)
        for d in range(D):
            for b in range(R):
                scaled[b * TB:(b + 1) * TB, :] = (
                    columns[d, :, k * R + b:k * R + b + 1] * on_all[d, b][:, F:].astype(f32)
                ).astype(bf16)
            moved = moved + lax.dot_general(
                scaled[...], slopes[k, d * R * TB:(d + 1) * R * TB, :], first,
                preferred_element_type=f32)
        term = lax.dot_general(moved.astype(bf16), w16[k], last, preferred_element_type=f32)

        @pl.when(lo == 0)
        def _():
            ga_own[k] = term[:, :F2]
            ga_out[k] = term[:, F2:].astype(bf16)

        @pl.when(lo == 1)
        def _():
            ga_own[k] = term[:, F2:]
            ga_out[k] = term[:, :F2].astype(bf16)
        ga_copy(k).start()

    def er_copy(c):
        return copy(err_top, err_top, er_s.at[c - 1], er_r.at[c - 1], col=(col + c) % C)

    def gh_copy(x):
        c, d = plane[x]
        return copy(gh.at[dp], gh.at[dp], gh_s.at[x], gh_r.at[x],
                    col=(col + c) % C, dp=(dp + d) % D)

    slot = lax.broadcasted_iota(jnp.int32, (2 * R, H), 0)

    @pl.when(col == 0)
    def _():
        err_top[...] = err_own[dp]
        for c in range(1, C):
            er_copy(c).start()
        twice = (2.0 * err_own[dp]).astype(bf16)
        total = jnp.zeros((2 * R, H), f32)
        for k in range(2):
            for b in range(R):
                got = jnp.dot(twice, hidden[k, b * TB:(b + 1) * TB, :],
                              preferred_element_type=f32)
                total = total + jnp.where(slot == k * R + b, got, 0.0)
        gh[dp] = total
        for x in range(len(plane)):
            gh_copy(x).start()

    for k in range(2):
        ga_copy(k).wait_recv()
        gb_all[k, hi] = (ga_own[k] + ga_in[k].astype(f32)).astype(bf16)
        for o in range(1, HI):
            gb_copy(k, o).start()

    def blend(fresh, target):
        return blend_rate * fresh + (1.0 - blend_rate) * target

    def grad_in(k):
        def scale(d):
            for b in range(R):
                at = pl.ds(pl.multiple_of((d * R + b) * TB, TB), TB)
                delta[b * TB:(b + 1) * TB, :] = (
                    columns[d, :, k * R + b:k * R + b + 1] * slopes[k, at, :].astype(f32)
                ).astype(bf16)
            at = pl.ds(pl.multiple_of(d * R * TB, R * TB), R * TB)
            return lax.dot_general(emb[k, at, :], delta[...], first, preferred_element_type=f32)

        def add(d, carry):
            new_in[k] += scale(d)
            return carry
        new_in[k] = scale(0)
        lax.fori_loop(1, D, add, 0)
        fresh = cin[k] - matrix_rate * new_in[k]
        new_in[k] = fresh
        new_tin[k] = blend(fresh, tin[k])

    grad_in(0)
    grad_in(1)

    for k in range(2):
        for o in range(1, HI):
            gb_copy(k, o).wait_recv()
        piece = gb_all[k, 0].astype(f32)
        for h in range(1, HI):
            piece = piece + gb_all[k, h].astype(f32)
        gc_all[k, lo] = piece.astype(bf16)
        gc_copy(k).start()

    for c in range(1, C):
        pz_copy(c).wait_recv()
    push = pz_all[0].astype(f32)
    for c in range(1, C):
        push = push + pz_all[c].astype(f32)
    epad[0:1, :] = flags[...].astype(f32)
    flag_column[...] = epad[...].T[:, 0:1]
    push_out[...] = push * flag_column[...]

    for c in range(1, C):
        @pl.when(col == c)
        def _():
            er_copy(c).wait_recv()
    for k in range(2):
        errs_out[k:k + 1, :] = err_top[pl.ds(k * R + row, 1), :]

    for x, (c, d) in enumerate(plane):
        @pl.when(col == c)
        def _():
            gh_copy(x).wait_recv()
    whole = gh[0]
    for d in range(1, D):
        whole = whole + gh[d]
    for k in range(2):
        grad = jnp.sum(whole[k * R:(k + 1) * R], axis=0, keepdims=True)
        fresh = chead[k:k + 1, :] - head_rate * grad
        new_head[k:k + 1, :] = fresh
        new_thead[k:k + 1, :] = blend(fresh, thead[k:k + 1, :])

    for k in range(2):
        gc_copy(k).wait_recv()
        for p in range(2):
            part = slice(p * F2, (p + 1) * F2)
            fresh = cact[k, :, part] - matrix_rate * gc_all[k, p].astype(f32)
            new_act[k, :, part] = fresh
            new_tact[k, :, part] = blend(fresh, tact[k, :, part])

    for o in range(HI):
        tg_copy(o).wait_send()
        if o > 0:
            ftg_copy(o, row).wait_send()
    for o in range(1, R):
        on_copy(o).wait_send()
        rd_copy(o).wait_send()
        pu_copy(o).wait_send()
        for e in range(1, D):
            oo_copy(e, o).wait_send()
    for e in range(1, D):
        ox_copy(e).wait_send()
    for a in range(2):
        far = col if a == 0 else C - 1 - col

        @pl.when(far < C - 1)
        def _():
            def left(i, carry):
                tr_copy(a, i).wait_send()
                return carry
            lax.fori_loop(0, nt, left, 0)

            def gone(q, carry):
                or_copy(a, q).wait_send()
                return carry
            lax.fori_loop(0, no, gone, 0)

        @pl.when(far == C - 1)
        def _():
            for o in range(1, R):
                vt_copy(o).wait_send()
            for x in range(len(plane)):
                gl_copy(x, a).wait_send()

    def away(q, carry):
        for e in range(1, D):
            xs_copy(q, e).wait_send()
        return carry
    lax.fori_loop(0, no, away, 0)
    for x in range(len(group)):
        vo_copy(x).wait_send()
    for c in range(1, C):
        pz_copy(c).wait_send()

    @pl.when(col == 0)
    def _():
        for c in range(1, C):
            er_copy(c).wait_send()
        for x in range(len(plane)):
            gh_copy(x).wait_send()
    for k in range(2):
        ga_copy(k).wait_send()
        gc_copy(k).wait_send()
        for o in range(1, HI):
            gb_copy(k, o).wait_send()


def put_out(*refs):
    count = len(refs) // 2
    copies = [pltpu.make_async_copy(refs[x], refs[count + x], refs[-1].at[x])
              for x in range(count)]
    for one in copies:
        one.start()
    for one in copies:
        one.wait()


def on_device(dims, observed, next_observed, actions, next_mean, policy_noise, rewards, discounts,
              actor_flags, critic_in, critic_act, critic_head, target_in, target_act, target_head):
    R, C, D, TB, F, H, A = dims
    HI, TC = R // 2, TB // pieces
    nt, no = 2 * HI * pieces, 2 * R * pieces
    planes, groups = C * D - 1, R * D - 1
    dma = lambda *shape: pltpu.SemaphoreType.DMA(shape)
    vmem = pltpu.VMEM
    scratch = [
        vmem((TB, A), bf16), vmem((TB, A), f32), vmem((1, TB), bf16), vmem((1, TB), bf16),
        vmem((1, TB), jnp.int32), vmem((2, F, H), f32), vmem((2, A, F), f32), vmem((2, H), f32),
        vmem((2, F, H), f32), vmem((2, A, F), f32), vmem((2, H), f32),
        vmem((TB, F + A), bf16), vmem((TB, F + A), bf16), vmem((TB, 1), f32),
        vmem((4, F, H), bf16), vmem((4, A, F), bf16),
        vmem((D, R, TB, F + A), bf16), vmem((R, TB, F + A), bf16),
        vmem((2, (D + 1) * R * TB, F), bf16),
        vmem((2, D * R * TB, H), bf16), vmem((R * TB, H), bf16), vmem((A, H), bf16),
        vmem((2, nt, TC, H), bf16), vmem((2, nt, TC, H), bf16),
        vmem((2, no, TC, H), bf16), vmem((2, no, TC, H), bf16),
        vmem((2, R * TB, H), bf16), vmem((TB, 128), f32), vmem((TB, 128), f32),
        vmem((8, TB), f32), vmem((R, 8, TB), f32), vmem((R, 2 * R, TB), f32),
        vmem((D, R, 2 * R, TB), f32), vmem((D, 2, 2 * R, TB), f32),
        vmem((D, 2 * R, TB), f32), vmem((2 * R, TB), f32), vmem((D, 2 * R, H), f32),
        vmem((128, TB), f32), vmem((D, TB, 128), f32), vmem((R * TB, A), bf16),
        vmem((2, A, F // 2), f32), vmem((2, A, F // 2), bf16), vmem((2, A, F // 2), bf16),
        vmem((2, HI, A, F // 2), bf16), vmem((2, 2, A, F // 2), bf16),
        vmem((R - 1, TB, A), bf16), vmem((R - 1, TB, A), bf16), vmem((C, TB, A), bf16),
        dma(16),
        dma(R - 1), dma(R - 1), dma(HI), dma(HI), dma(HI), dma(HI),
        dma(D - 1), dma(D - 1), dma(D - 1, R - 1), dma(D - 1, R - 1), dma(R - 1), dma(R - 1),
        dma(2, nt), dma(2, nt), dma(2, no), dma(2, no), dma(no, D - 1), dma(no, D - 1),
        dma(R - 1), dma(R - 1), dma(groups), dma(groups), dma(planes), dma(2, planes),
        dma(C - 1), dma(C - 1), dma(planes), dma(planes),
        dma(2), dma(2), dma(2, HI - 1), dma(2, HI - 1), dma(2), dma(2),
        dma(R - 1), dma(R - 1), dma(C - 1), dma(C - 1),
    ]
    spec = pl.BlockSpec(memory_space=vmem)
    results = (((2, F, H), f32), ((2, A, F), f32), ((2, H), f32), ((2, F, H), f32),
               ((2, A, F), f32), ((2, H), f32), ((2, TB), f32), ((TB, A), f32))
    kept = pl.pallas_call(
        functools.partial(kernel, dims),
        out_shape=tuple(vmem(shape, kind) for shape, kind in results),
        in_specs=[pl.BlockSpec(memory_space=pltpu.HBM)] * 14,
        out_specs=(spec,) * len(results),
        scratch_shapes=scratch,
        compiler_params=pltpu.CompilerParams(
            collective_id=0, has_side_effects=True, vmem_limit_bytes=57 * 2 ** 20),
    )(*[pltpu.with_memory_space_constraint(one, pltpu.HBM) for one in (
        observed, next_observed, actions, next_mean, policy_noise, rewards[None, :],
        discounts[None, :], actor_flags[None, :], critic_in, critic_act, critic_head, target_in,
        target_act, target_head)])
    return pl.pallas_call(
        put_out,
        out_shape=tuple(jax.ShapeDtypeStruct(shape, kind) for shape, kind in results),
        in_specs=[spec] * len(results),
        out_specs=(pl.BlockSpec(memory_space=pl.ANY),) * len(results),
        scratch_shapes=[dma(len(results))],
        compiler_params=pltpu.CompilerParams(vmem_limit_bytes=12 * 2 ** 20),
    )(*[pltpu.with_memory_space_constraint(one, vmem) for one in kept])


def solution(mesh):
    def run(*args):
        R, C, D = mesh.shape["row"], mesh.shape["col"], mesh.shape["dp"]
        tokens, features = args[0].shape
        dims = (R, C, D, tokens // (R * D), features // C, args[8].shape[2] // R,
                args[2].shape[1])
        return sharded(dims)(*args)

    def sharded(dims):
        return jax.shard_map(
            functools.partial(on_device, dims),
            mesh=mesh,
            in_specs=(
                P(("row", "dp"), "col"),
                P(("row", "dp"), "col"),
                P(("row", "dp"), None),
                P(("row", "dp"), None),
                P(("row", "dp"), None),
                P(("row", "dp")),
                P(("row", "dp")),
                P(("row", "dp")),
                P(None, "col", "row"),
                P(None, None, "col"),
                P(None, "row"),
                P(None, "col", "row"),
                P(None, None, "col"),
                P(None, "row"),
            ),
            out_specs=(
                P(None, "col", "row"),
                P(None, None, "col"),
                P(None, "row"),
                P(None, "col", "row"),
                P(None, None, "col"),
                P(None, "row"),
                P(None, ("row", "dp")),
                P(("row", "dp"), None),
            ),
            check_vma=False,
        )

    return run
```

time: 78.6 us -> 73.9 us (0.940)
  Pallas kernels: 77.2 us -> 72.8 us
    pallas_call x1, Pallas kernels: 74.8 us -> 70.4 us  [on_device(): pl.pallas_call(functools.partial(kernel, dims), out_shape=tuple((vmem(sha...]
where the time goes in v2:
time: 73.9 us; the launch traced here: 73.5 us
  Pallas kernels  72.8 us (99%)
    pallas_call x1, Pallas kernels, on_device(): pl.pallas_call(functools.partial(kernel, dims), out_shape=tuple((vmem(sha...  70.4 us
    pallas_call x1, Pallas kernels, on_device(): pl.pallas_call(put_out, out_shape=tuple((jax.ShapeDtypeStruct(shape, kind...  2.43 us

profile of v2, /device:TPU:0, one launch (start us, length us, event | category | flops | bytes accessed | tf_op | source)
XLA Modules:
  0.0 73.5 jit_solution(13649700118127695381)
XLA Ops:
  0.6 70.4 %shard_map.197 = (f32[2,512,512]{2,1,0:T(8,128)S(1)}, f32[2,128,512]{2,1,0:T(8,128)S(1)}, f32[2,512]{1,0:T(2,128)S(1)}, f32[2,512,512]{2,1,0:T(8,128)S(1)}, f32[...) custom-call(bf16[128,512]{1,0:T(8,128)(2,1)} %observed_at.1, ...), custom_call_target="tpu_custom_call" | custom-call | tf_op jit(solution)/shard_map/pallas_call | solution.py:656
  71.0 2.4 %shard_map.198 = (f32[2,512,512]{2,1,0:T(8,128)}, f32[2,128,512]{2,1,0:T(8,128)}, f32[2,512]{1,0:T(2,128)}, f32[2,512,512]{2,1,0:T(8,128)}, f32[2,128,512]{2,1,0...) custom-call(f32[2,512,512]{2,1,0:T(8,128)S(1)} %get-tuple-element.16.refs_0_, ...), custom_call_target="tpu_custom_call" | custom-call | tf_op jit(solution)/shard_map/pallas_call | solution.py:668

commit v3 on v2

--- a/solution.py
+++ b/solution.py
@@ -15,6 +15,7 @@
 f32 = jnp.float32
 bf16 = jnp.bfloat16
 skew = 3
+lead = 2
 pieces = 2
 
 
@@ -23,11 +24,11 @@
            new_in, new_act, new_head, new_tin, new_tact, new_thead, errs_out, push_out,
            next_mean, noise, rewards, discounts, flags, cin, cact, chead, tin, tact, thead,
            on_own, tg_own, flag_column, w16, a16, on_all, tg_all, emb, slopes, delta, lift,
-           t_out, t_in, o_out, o_in, hidden, vals_t, vals_o, rd_own, rd_all, vt_all, vo_all, gl,
+           sums_out, sums_in, mine, hidden, vals_t, vals_o, rd_own, rd_all, vt_all, vo_all, gl,
            err_own, err_top, gh, epad, columns, scaled,
            ga_own, ga_out, ga_in, gb_all, gc_all, pu_out, pu_in, pz_all,
            load_s, on_s, on_r, tg_s, tg_r, ftg_s, ftg_r, ox_s, ox_r, oo_s, oo_r, rd_s, rd_r,
-           tr_s, tr_r, or_s, or_r, xs_s, xs_r, vt_s, vt_r, vo_s, vo_r, gl_s, gl_r, er_s, er_r,
+           sm_s, sm_r, xs_s, xs_r, vt_s, vt_r, vo_s, vo_r, gl_s, gl_r, er_s, er_r,
            gh_s, gh_r, ga_s, ga_r, gb_s, gb_r, gc_s, gc_r, pu_s, pu_r, pz_s, pz_r):
     R, C, D, TB, F, H, A = dims
     HI = R // 2
@@ -36,6 +37,7 @@
     hi, lo = row // 2, row % 2
     nt = 2 * HI * pieces
     no = 2 * R * pieces
+    n = nt + no
     partner = hi * 2 + (1 - lo)
 
     def copy(src, dst, ssem, rsem, **where):
@@ -96,23 +98,26 @@
     for o in range(HI):
         tg_copy(o).start()
     tg_all[row] = tg_own[...]
+    for x in range(9, 11):
+        loads[x].wait()
+    rd_own[...] = jnp.zeros_like(rd_own)
+    rd_own[0:1, :] = rewards[...].astype(f32)
+    rd_own[1:2, :] = discounts[...].astype(f32)
+    for o in range(1, R):
+        rd_copy(o).start()
+    rd_all[row] = rd_own[...]
     for x in range(3, 7):
         loads[x].wait()
     for k in range(2):
         a16[2 + k] = tact[k].astype(bf16)
         w16[2 + k] = tin[k].astype(bf16)
-    for x in range(7, 12):
+    for x in (7, 8):
         loads[x].wait()
     for e in range(1, D):
         ox_copy(e).start()
-    rd_own[...] = jnp.zeros_like(rd_own)
-    rd_own[0:1, :] = rewards[...].astype(f32)
-    rd_own[1:2, :] = discounts[...].astype(f32)
     for o in range(1, R):
         on_copy(o).start()
-        rd_copy(o).start()
     on_all[dp, row] = on_own[...]
-    rd_all[row] = rd_own[...]
 
     def rows_of(d, block):
         return pl.ds(pl.multiple_of((d * R + block) * TB, TB), TB)
@@ -135,12 +140,6 @@
 
             @pl.when(i == 2 * pieces * o)
             def _():
-                @pl.when(lo == a)
-                def _():
-                    if o > 0:
-                        tg_copy(o).wait_recv()
-                        ftg_copy(o, block).start()
-
                 @pl.when(lo != a)
                 def _():
                     if o > 0:
@@ -149,6 +148,13 @@
                         tg_copy(0).wait_recv()
                 embed_tg(block)
 
+    def forward_tg(a, i):
+        for o in range(1, HI):
+            @pl.when((i == 2 * pieces * o - 1) & (lo == a))
+            def _():
+                tg_copy(o).wait_recv()
+                ftg_copy(o, ((hi + HI - o) % HI) * 2 + a).start()
+
     def prepare_on(q):
         for o in range(R):
             @pl.when(q == 2 * pieces * o)
@@ -160,11 +166,11 @@
     def along(a):
         return (col + 1) % C if a == 0 else (col + C - 1) % C
 
-    def tr_copy(a, i):
-        return copy(t_out.at[a, i], t_in.at[a, i], tr_s.at[a, i], tr_r.at[a, i], col=along(a))
-
-    def or_copy(a, q):
-        return copy(o_out.at[a, q], o_in.at[a, q], or_s.at[a, q], or_r.at[a, q], col=along(a))
+    def sm_copy(a, i):
+        return copy(sums_out.at[a, i], sums_in.at[a, i], sm_s.at[a], sm_r.at[a, i], col=along(a))
+
+    def sm_sent(a):
+        return copy(sums_out.at[a], sums_in.at[a], sm_s.at[a], sm_r.at[a, 0], col=along(a))
 
     def place_t(a, i):
         block = ((hi + HI - i // (2 * pieces)) % HI) * 2 + a
@@ -179,7 +185,11 @@
     def xs_copy(q, e):
         block, kk, piece = place_o(q)
         at = slopes.at[kk, chunk(dp, block, piece), :]
-        return copy(at, at, xs_s.at[q, e - 1], xs_r.at[q, e - 1], dp=(dp + e) % D)
+        return copy(at, at, xs_s.at[e - 1], xs_r.at[e - 1], dp=(dp + e) % D)
+
+    def xs_whole(e):
+        at = slopes.at[:, pl.ds(pl.multiple_of(dp * R * TB, R * TB), R * TB), :]
+        return copy(at, at, xs_s.at[e - 1], xs_r.at[e - 1], dp=(dp + e) % D)
 
     def vt_copy(o):
         return copy(vt_all.at[row], vt_all.at[row], vt_s.at[o - 1], vt_r.at[o - 1],
@@ -225,7 +235,7 @@
             for o in range(1, R):
                 vt_copy(o).start()
 
-        @pl.when(i == nt + 3)
+        @pl.when(i == nt + 2 * pieces - 1)
         def _():
             for o in range(1, R):
                 vt_copy(o).wait_recv()
@@ -241,23 +251,26 @@
             for x in range(len(plane)):
                 gl_copy(x, a).start()
 
-    steps = nt + no + skew * (C - 1)
+    def later(a, far):
+        return 2 * far > C - 1 if a == 0 else 2 * far >= C - 1
+
+    steps = n + lead + skew * (C - 1)
 
     def aside(s):
         @pl.when(s == 1)
         def _():
-            for x in range(12, 16):
+            for x in range(11, 16):
                 loads[x].wait()
             for k in range(2):
                 a16[k] = cact[k].astype(bf16)
                 w16[k] = cin[k].astype(bf16)
 
-        @pl.when(s == 4)
+        @pl.when(s == nt)
         def _():
             for o in range(1, R):
                 rd_copy(o).wait_recv()
 
-        @pl.when(s == nt)
+        @pl.when(s == nt + 2)
         def _():
             for e in range(1, D):
                 ox_copy(e).wait_recv()
@@ -277,73 +290,68 @@
                     embed_on((dp + D - e) % D, (row + R - o) % R)
 
     def step(s, carry):
+        at = []
         for a in range(2):
             far = col if a == 0 else C - 1 - col
-            i = s - skew * far
-
-            @pl.when((i >= 0) & (i < nt))
-            def _():
-                prepare_tg(a, i)
-                block, kk, piece = place_t(a, i)
-
-                def partial():
-                    return jnp.dot(emb[kk, chunk(D, block, piece), :], w16[2 + kk],
-                                   preferred_element_type=f32)
-
-                @pl.when(far == 0)
+            i = s - skew * far - jnp.where(far > 0, lead, 0)
+            at.append((a, far, i, (i >= 0) & (i < n)))
+
+        for a, far, i, live in at:
+            @pl.when(live)
+            def _():
+                early = i < nt
+                q = i - nt
+                tb, tk, tp = place_t(a, i)
+                ob, ok, op = place_o(jnp.maximum(q, 0))
+                kk = jnp.where(early, tk, ok)
+                start = (jnp.where(early, D * R + tb, dp * R + ob) * TB
+                         + jnp.where(early, tp, op) * TC)
+
+                @pl.when(early)
                 def _():
-                    t_out[a, i] = partial().astype(bf16)
-                    tr_copy(a, i).start()
-
-                @pl.when((far > 0) & (far < C - 1))
+                    prepare_tg(a, i)
+
+                @pl.when((q >= 0) & jnp.logical_not(later(a, far)))
                 def _():
-                    mine = partial()
-                    tr_copy(a, i).wait_recv()
-                    t_out[a, i] = (mine + t_in[a, i].astype(f32)).astype(bf16)
-                    tr_copy(a, i).start()
-
+                    prepare_on(q)
+                mine[a] = jnp.dot(emb[kk, pl.ds(pl.multiple_of(start, TC), TC), :],
+                                  w16[jnp.where(early, 2, 0) + kk],
+                                  preferred_element_type=f32)
+
+        for a, far, i, live in at:
+            @pl.when(live & (far == 0))
+            def _():
+                sums_out[a, i] = mine[a].astype(bf16)
+                sm_copy(a, i).start()
+
+        for a, far, i, live in at:
+            @pl.when(live & (far > 0) & (far < C - 1))
+            def _():
+                sm_copy(a, i).wait_recv()
+                total = mine[a] + sums_in[a, i].astype(f32)
+                sums_out[a, i] = total.astype(bf16)
+                sm_copy(a, i).start()
+                mine[a] = total
+
+            @pl.when(live & (far == C - 1))
+            def _():
+                sm_copy(a, i).wait_recv()
+                mine[a] += sums_in[a, i].astype(f32)
+
+        for a, far, i, live in at:
+            @pl.when(live & (i < nt))
+            def _():
                 @pl.when(far == C - 1)
                 def _():
-                    mine = partial()
-                    tr_copy(a, i).wait_recv()
-                    finish_t(a, i, mine + t_in[a, i].astype(f32))
-
-            @pl.when((i >= nt) & (i < nt + no))
-            def _():
-                q = i - nt
-                block, kk, piece = place_o(q)
-                later = 2 * far > C - 1 if a == 0 else 2 * far >= C - 1
-
-                @pl.when(jnp.logical_not(later))
+                    finish_t(a, i, mine[a])
+                forward_tg(a, i)
+
+            @pl.when(live & (i >= nt) & later(a, far))
+            def _():
+                @pl.when(far < C - 1)
                 def _():
-                    prepare_on(q)
-
-                def partial():
-                    return jnp.dot(emb[kk, chunk(dp, block, piece), :], w16[kk],
-                                   preferred_element_type=f32)
-
-                @pl.when(far == 0)
-                def _():
-                    o_out[a, q] = partial().astype(bf16)
-                    or_copy(a, q).start()
-
-                @pl.when((far > 0) & (far < C - 1))
-                def _():
-                    mine = partial()
-                    or_copy(a, q).wait_recv()
-                    mine = mine + o_in[a, q].astype(f32)
-                    o_out[a, q] = mine.astype(bf16)
-                    or_copy(a, q).start()
-
-                    @pl.when(later)
-                    def _():
-                        finish_o(q, mine + o_in[1 - a, q].astype(f32))
-
-                @pl.when(far == C - 1)
-                def _():
-                    mine = partial()
-                    or_copy(a, q).wait_recv()
-                    finish_o(q, mine + o_in[a, q].astype(f32))
+                    mine[a] += sums_in[1 - a, i].astype(f32)
+                finish_o(i - nt, mine[a])
 
             @pl.when(far == C - 1)
             def _():
@@ -367,12 +375,11 @@
 
     last = (((1,), (1,)), ((), ()))
     first = (((0,), (0,)), ((), ()))
-    own_push = None
     for o in list(range(1, R)) + [0]:
         got = lax.dot_general(slopes[0, rows_of(dp, (row + o) % R), :], lift[...], last,
                               preferred_element_type=f32)
         if o == 0:
-            own_push = got
+            push_out[...] = got
         else:
             pu_out[o - 1] = got.astype(bf16)
             pu_copy(o).start()
@@ -384,18 +391,8 @@
             def _():
                 gl_copy(x, a).wait_recv()
 
-    for o in range(1, R):
-        pu_copy(o).wait_recv()
-        own_push = own_push + pu_in[o - 1].astype(f32)
-    pz_all[col] = own_push.astype(bf16)
-    for c in range(1, C):
-        pz_copy(c).start()
-
     for e in range(1, D):
-        def take(q, carry):
-            xs_copy(q, e).wait_recv()
-            return carry
-        lax.fori_loop(0, no, take, 0)
+        xs_whole(e).wait_recv()
     for x in range(len(group)):
         vo_copy(x).wait_recv()
 
@@ -412,7 +409,7 @@
     F2 = F // 2
 
     def ga_copy(k):
-        return copy(ga_out.at[k], ga_in.at[k], ga_s.at[k], ga_r.at[k], row=partner)
+        return copy(ga_out.at[k, 1 - lo], ga_in.at[k], ga_s.at[k], ga_r.at[k], row=partner)
 
     def gb_copy(k, o):
         return copy(gb_all.at[k, hi], gb_all.at[k, hi], gb_s.at[k, o - 1], gb_r.at[k, o - 1],
@@ -421,28 +418,7 @@
     def gc_copy(k):
         return copy(gc_all.at[k, lo], gc_all.at[k, lo], gc_s.at[k], gc_r.at[k], row=partner)
 
-    for k in range(2):
-        moved = jnp.zeros((A, H), f32)
-        for d in range(D):
-            for b in range(R):
-                scaled[b * TB:(b + 1) * TB, :] = (
-                    columns[d, :, k * R + b:k * R + b + 1] * on_all[d, b][:, F:].astype(f32)
-                ).astype(bf16)
-            moved = moved + lax.dot_general(
-                scaled[...], slopes[k, d * R * TB:(d + 1) * R * TB, :], first,
-                preferred_element_type=f32)
-        term = lax.dot_general(moved.astype(bf16), w16[k], last, preferred_element_type=f32)
-
-        @pl.when(lo == 0)
-        def _():
-            ga_own[k] = term[:, :F2]
-            ga_out[k] = term[:, F2:].astype(bf16)
-
-        @pl.when(lo == 1)
-        def _():
-            ga_own[k] = term[:, F2:]
-            ga_out[k] = term[:, :F2].astype(bf16)
-        ga_copy(k).start()
+    chief = 1 % C
 
     def er_copy(c):
         return copy(err_top, err_top, er_s.at[c - 1], er_r.at[c - 1], col=(col + c) % C)
@@ -454,7 +430,7 @@
 
     slot = lax.broadcasted_iota(jnp.int32, (2 * R, H), 0)
 
-    @pl.when(col == 0)
+    @pl.when(col == chief)
     def _():
         err_top[...] = err_own[dp]
         for c in range(1, C):
@@ -471,10 +447,34 @@
             gh_copy(x).start()
 
     for k in range(2):
+        moved = jnp.zeros((A, H), f32)
+        for d in range(D):
+            for b in range(R):
+                scaled[b * TB:(b + 1) * TB, :] = (
+                    columns[d, :, k * R + b:k * R + b + 1] * on_all[d, b][:, F:].astype(f32)
+                ).astype(bf16)
+            moved = moved + lax.dot_general(
+                scaled[...], slopes[k, d * R * TB:(d + 1) * R * TB, :], first,
+                preferred_element_type=f32)
+        term = lax.dot_general(moved.astype(bf16), w16[k], last, preferred_element_type=f32)
+
+        for p in range(2):
+            ga_own[k, p] = term[:, p * F2:(p + 1) * F2]
+            ga_out[k, p] = term[:, p * F2:(p + 1) * F2].astype(bf16)
+        ga_copy(k).start()
+
+    for k in range(2):
         ga_copy(k).wait_recv()
-        gb_all[k, hi] = (ga_own[k] + ga_in[k].astype(f32)).astype(bf16)
+        gb_all[k, hi] = (ga_own[k, lo] + ga_in[k].astype(f32)).astype(bf16)
         for o in range(1, HI):
             gb_copy(k, o).start()
+
+    for o in range(1, R):
+        pu_copy(o).wait_recv()
+        push_out[...] += pu_in[o - 1].astype(f32)
+    pz_all[col] = push_out[...].astype(bf16)
+    for c in range(1, C):
+        pz_copy(c).start()
 
     def blend(fresh, target):
         return blend_rate * fresh + (1.0 - blend_rate) * target
@@ -520,14 +520,14 @@
     push_out[...] = push * flag_column[...]
 
     for c in range(1, C):
-        @pl.when(col == c)
+        @pl.when(col == (chief + c) % C)
         def _():
             er_copy(c).wait_recv()
     for k in range(2):
         errs_out[k:k + 1, :] = err_top[pl.ds(k * R + row, 1), :]
 
     for x, (c, d) in enumerate(plane):
-        @pl.when(col == c)
+        @pl.when(col == (chief + c) % C)
         def _():
             gh_copy(x).wait_recv()
     whole = gh[0]
@@ -564,15 +564,7 @@
 
         @pl.when(far < C - 1)
         def _():
-            def left(i, carry):
-                tr_copy(a, i).wait_send()
-                return carry
-            lax.fori_loop(0, nt, left, 0)
-
-            def gone(q, carry):
-                or_copy(a, q).wait_send()
-                return carry
-            lax.fori_loop(0, no, gone, 0)
+            sm_sent(a).wait_send()
 
         @pl.when(far == C - 1)
         def _():
@@ -581,17 +573,14 @@
             for x in range(len(plane)):
                 gl_copy(x, a).wait_send()
 
-    def away(q, carry):
-        for e in range(1, D):
-            xs_copy(q, e).wait_send()
-        return carry
-    lax.fori_loop(0, no, away, 0)
+    for e in range(1, D):
+        xs_whole(e).wait_send()
     for x in range(len(group)):
         vo_copy(x).wait_send()
     for c in range(1, C):
         pz_copy(c).wait_send()
 
-    @pl.when(col == 0)
+    @pl.when(col == chief)
     def _():
         for c in range(1, C):
             er_copy(c).wait_send()
@@ -631,20 +620,19 @@
         vmem((D, R, TB, F + A), bf16), vmem((R, TB, F + A), bf16),
         vmem((2, (D + 1) * R * TB, F), bf16),
         vmem((2, D * R * TB, H), bf16), vmem((R * TB, H), bf16), vmem((A, H), bf16),
-        vmem((2, nt, TC, H), bf16), vmem((2, nt, TC, H), bf16),
-        vmem((2, no, TC, H), bf16), vmem((2, no, TC, H), bf16),
+        vmem((2, nt + no, TC, H), bf16), vmem((2, nt + no, TC, H), bf16), vmem((2, TC, H), f32),
         vmem((2, R * TB, H), bf16), vmem((TB, 128), f32), vmem((TB, 128), f32),
         vmem((8, TB), f32), vmem((R, 8, TB), f32), vmem((R, 2 * R, TB), f32),
         vmem((D, R, 2 * R, TB), f32), vmem((D, 2, 2 * R, TB), f32),
         vmem((D, 2 * R, TB), f32), vmem((2 * R, TB), f32), vmem((D, 2 * R, H), f32),
         vmem((128, TB), f32), vmem((D, TB, 128), f32), vmem((R * TB, A), bf16),
-        vmem((2, A, F // 2), f32), vmem((2, A, F // 2), bf16), vmem((2, A, F // 2), bf16),
+        vmem((2, 2, A, F // 2), f32), vmem((2, 2, A, F // 2), bf16), vmem((2, A, F // 2), bf16),
         vmem((2, HI, A, F // 2), bf16), vmem((2, 2, A, F // 2), bf16),
         vmem((R - 1, TB, A), bf16), vmem((R - 1, TB, A), bf16), vmem((C, TB, A), bf16),
         dma(16),
         dma(R - 1), dma(R - 1), dma(HI), dma(HI), dma(HI), dma(HI),
         dma(D - 1), dma(D - 1), dma(D - 1, R - 1), dma(D - 1, R - 1), dma(R - 1), dma(R - 1),
-        dma(2, nt), dma(2, nt), dma(2, no), dma(2, no), dma(no, D - 1), dma(no, D - 1),
+        dma(2), dma(2, nt + no), dma(D - 1), dma(D - 1),
         dma(R - 1), dma(R - 1), dma(groups), dma(groups), dma(planes), dma(2, planes),
         dma(C - 1), dma(C - 1), dma(planes), dma(planes),
         dma(2), dma(2), dma(2, HI - 1), dma(2, HI - 1), dma(2), dma(2),

time: 73.9 us -> 68.8 us (0.931)
  Pallas kernels: 72.8 us -> 68 us
    pallas_call x1, Pallas kernels: 70.4 us -> 65.6 us  [on_device(): pl.pallas_call(functools.partial(kernel, dims), out_shape=tuple((vmem(sha...]
where the time goes in v3:
time: 68.8 us; the launch traced here: 68.6 us
  Pallas kernels  68 us (99%)
    pallas_call x1, Pallas kernels, on_device(): pl.pallas_call(functools.partial(kernel, dims), out_shape=tuple((vmem(sha...  65.6 us
    pallas_call x1, Pallas kernels, on_device(): pl.pallas_call(put_out, out_shape=tuple((jax.ShapeDtypeStruct(shape, kind...  2.43 us

profile of v3, /device:TPU:0, one launch (start us, length us, event | category | flops | bytes accessed | tf_op | source)
XLA Modules:
  0.0 68.6 jit_solution(275563418352252083)
XLA Ops:
  0.6 65.6 %shard_map.197 = (f32[2,512,512]{2,1,0:T(8,128)S(1)}, f32[2,128,512]{2,1,0:T(8,128)S(1)}, f32[2,512]{1,0:T(2,128)S(1)}, f32[2,512,512]{2,1,0:T(8,128)S(1)}, f32[...) custom-call(bf16[128,512]{1,0:T(8,128)(2,1)} %observed_at.1, ...), custom_call_target="tpu_custom_call" | custom-call | tf_op jit(solution)/shard_map/pallas_call | solution.py:644
  66.2 2.4 %shard_map.198 = (f32[2,512,512]{2,1,0:T(8,128)}, f32[2,128,512]{2,1,0:T(8,128)}, f32[2,512]{1,0:T(2,128)}, f32[2,512,512]{2,1,0:T(8,128)}, f32[2,128,512]{2,1,0...) custom-call(f32[2,512,512]{2,1,0:T(8,128)S(1)} %get-tuple-element.16.refs_0_, ...), custom_call_target="tpu_custom_call" | custom-call | tf_op jit(solution)/shard_map/pallas_call | solution.py:656

commit v4 on v3

--- a/solution.py
+++ b/solution.py
@@ -14,7 +14,7 @@
 
 f32 = jnp.float32
 bf16 = jnp.bfloat16
-skew = 3
+pace = 5
 lead = 2
 pieces = 2
 
@@ -23,9 +23,9 @@
            discounts_at, flags_at, cin_at, cact_at, chead_at, tin_at, tact_at, thead_at,
            new_in, new_act, new_head, new_tin, new_tact, new_thead, errs_out, push_out,
            next_mean, noise, rewards, discounts, flags, cin, cact, chead, tin, tact, thead,
-           on_own, tg_own, flag_column, w16, a16, on_all, tg_all, emb, slopes, delta, lift,
+           on_own, tg_own, flag_column, w16, a16, on_all, tg_all, emb, slopes, turned, lift,
            sums_out, sums_in, mine, hidden, vals_t, vals_o, rd_own, rd_all, vt_all, vo_all, gl,
-           err_own, err_top, gh, epad, columns, scaled,
+           err_own, err_top, gh, epad, columns,
            ga_own, ga_out, ga_in, gb_all, gc_all, pu_out, pu_in, pz_all,
            load_s, on_s, on_r, tg_s, tg_r, ftg_s, ftg_r, ox_s, ox_r, oo_s, oo_r, rd_s, rd_r,
            sm_s, sm_r, xs_s, xs_r, vt_s, vt_r, vo_s, vo_r, gl_s, gl_r, er_s, er_r,
@@ -124,6 +124,7 @@
 
     def embed_on(d, block):
         x = on_all[d, block]
+        turned[:, rows_of(d, block)] = x[:, F:].T
         for k in range(2):
             mixed = jnp.dot(x[:, F:], a16[k], preferred_element_type=f32)
             emb[k, rows_of(d, block), :] = (x[:, :F].astype(f32) + mixed).astype(bf16)
@@ -148,9 +149,9 @@
                         tg_copy(0).wait_recv()
                 embed_tg(block)
 
-    def forward_tg(a, i):
+    def forward_tg(a, i, far):
         for o in range(1, HI):
-            @pl.when((i == 2 * pieces * o - 1) & (lo == a))
+            @pl.when((i == 2 * pieces * o - jnp.where(far == 0, 1, pieces + 1)) & (lo == a))
             def _():
                 tg_copy(o).wait_recv()
                 ftg_copy(o, ((hi + HI - o) % HI) * 2 + a).start()
@@ -164,7 +165,7 @@
                 embed_on(dp, (row + R - o) % R)
 
     def along(a):
-        return (col + 1) % C if a == 0 else (col + C - 1) % C
+        return jnp.where(a == 0, col + 1, col + C - 1) % C
 
     def sm_copy(a, i):
         return copy(sums_out.at[a, i], sums_in.at[a, i], sm_s.at[a], sm_r.at[a, i], col=along(a))
@@ -185,11 +186,11 @@
     def xs_copy(q, e):
         block, kk, piece = place_o(q)
         at = slopes.at[kk, chunk(dp, block, piece), :]
-        return copy(at, at, xs_s.at[e - 1], xs_r.at[e - 1], dp=(dp + e) % D)
-
-    def xs_whole(e):
-        at = slopes.at[:, pl.ds(pl.multiple_of(dp * R * TB, R * TB), R * TB), :]
-        return copy(at, at, xs_s.at[e - 1], xs_r.at[e - 1], dp=(dp + e) % D)
+        return copy(at, at, xs_s.at[kk, e - 1], xs_r.at[kk, e - 1], dp=(dp + e) % D)
+
+    def xs_whole(k, e):
+        at = slopes.at[k, pl.ds(pl.multiple_of(dp * R * TB, R * TB), R * TB), :]
+        return copy(at, at, xs_s.at[k, e - 1], xs_r.at[k, e - 1], dp=(dp + e) % D)
 
     def vt_copy(o):
         return copy(vt_all.at[row], vt_all.at[row], vt_s.at[o - 1], vt_r.at[o - 1],
@@ -223,10 +224,16 @@
         head = chead[pl.ds(kk, 1), :]
         slopes[kk, chunk(dp, block, piece), :] = (
             head * (sigma * (1.0 + pre * (1.0 - sigma)))).astype(bf16)
+        hidden[kk, chunk(0, block, piece), :] = gate.astype(bf16)
+        note(vals_o, block, kk, piece, gate, head)
+
+        @pl.when(q == no - 1)
+        def _():
+            vo_all[dp, row] = vals_o[...].T[:2 * R]
+            for x in range(len(group)):
+                vo_copy(x).start()
         for e in range(1, D):
             xs_copy(q, e).start()
-        hidden[kk, chunk(0, block, piece), :] = gate.astype(bf16)
-        note(vals_o, block, kk, piece, gate, head)
 
     def settle(a, i):
         @pl.when(i == nt)
@@ -252,9 +259,9 @@
                 gl_copy(x, a).start()
 
     def later(a, far):
-        return 2 * far > C - 1 if a == 0 else 2 * far >= C - 1
-
-    steps = n + lead + skew * (C - 1)
+        return 2 * far + a > C - 1
+
+    steps = n + lead + pace * (C - 1) // 2
 
     def aside(s):
         @pl.when(s == 1)
@@ -291,9 +298,10 @@
 
     def step(s, carry):
         at = []
-        for a in range(2):
-            far = col if a == 0 else C - 1 - col
-            i = s - skew * far - jnp.where(far > 0, lead, 0)
+        for j in range(2):
+            a = (col + j) % 2
+            far = jnp.where(a == 0, col, C - 1 - col)
+            i = s - pace * far // 2 - jnp.where(far > 0, lead, 0)
             at.append((a, far, i, (i >= 0) & (i < n)))
 
         for a, far, i, live in at:
@@ -344,7 +352,7 @@
                 @pl.when(far == C - 1)
                 def _():
                     finish_t(a, i, mine[a])
-                forward_tg(a, i)
+                forward_tg(a, i, far)
 
             @pl.when(live & (i >= nt) & later(a, far))
             def _():
@@ -360,10 +368,6 @@
         return carry
 
     lax.fori_loop(0, steps, step, 0)
-
-    vo_all[dp, row] = vals_o[...].T[:2 * R]
-    for x in range(len(group)):
-        vo_copy(x).start()
 
     def pu_copy(o):
         return copy(pu_out.at[o - 1], pu_in.at[o - 1], pu_s.at[o - 1], pu_r.at[o - 1],
@@ -391,8 +395,6 @@
             def _():
                 gl_copy(x, a).wait_recv()
 
-    for e in range(1, D):
-        xs_whole(e).wait_recv()
     for x in range(len(group)):
         vo_copy(x).wait_recv()
 
@@ -447,15 +449,17 @@
             gh_copy(x).start()
 
     for k in range(2):
+        for e in range(1, D):
+            xs_whole(k, e).wait()
         moved = jnp.zeros((A, H), f32)
         for d in range(D):
             for b in range(R):
-                scaled[b * TB:(b + 1) * TB, :] = (
-                    columns[d, :, k * R + b:k * R + b + 1] * on_all[d, b][:, F:].astype(f32)
-                ).astype(bf16)
-            moved = moved + lax.dot_general(
-                scaled[...], slopes[k, d * R * TB:(d + 1) * R * TB, :], first,
-                preferred_element_type=f32)
+                at = slice((d * R + b) * TB, (d * R + b + 1) * TB)
+                slopes[k, at, :] = (columns[d, :, k * R + b:k * R + b + 1]
+                                    * slopes[k, at, :].astype(f32)).astype(bf16)
+            at = slice(d * R * TB, (d + 1) * R * TB)
+            moved = moved + jnp.dot(turned[:, at], slopes[k, at, :],
+                                    preferred_element_type=f32)
         term = lax.dot_general(moved.astype(bf16), w16[k], last, preferred_element_type=f32)
 
         for p in range(2):
@@ -480,19 +484,15 @@
         return blend_rate * fresh + (1.0 - blend_rate) * target
 
     def grad_in(k):
-        def scale(d):
-            for b in range(R):
-                at = pl.ds(pl.multiple_of((d * R + b) * TB, TB), TB)
-                delta[b * TB:(b + 1) * TB, :] = (
-                    columns[d, :, k * R + b:k * R + b + 1] * slopes[k, at, :].astype(f32)
-                ).astype(bf16)
+        def part(d):
             at = pl.ds(pl.multiple_of(d * R * TB, R * TB), R * TB)
-            return lax.dot_general(emb[k, at, :], delta[...], first, preferred_element_type=f32)
+            return lax.dot_general(emb[k, at, :], slopes[k, at, :], first,
+                                   preferred_element_type=f32)
 
         def add(d, carry):
-            new_in[k] += scale(d)
+            new_in[k] += part(d)
             return carry
-        new_in[k] = scale(0)
+        new_in[k] = part(0)
         lax.fori_loop(1, D, add, 0)
         fresh = cin[k] - matrix_rate * new_in[k]
         new_in[k] = fresh
@@ -573,8 +573,6 @@
             for x in range(len(plane)):
                 gl_copy(x, a).wait_send()
 
-    for e in range(1, D):
-        xs_whole(e).wait_send()
     for x in range(len(group)):
         vo_copy(x).wait_send()
     for c in range(1, C):
@@ -619,20 +617,20 @@
         vmem((4, F, H), bf16), vmem((4, A, F), bf16),
         vmem((D, R, TB, F + A), bf16), vmem((R, TB, F + A), bf16),
         vmem((2, (D + 1) * R * TB, F), bf16),
-        vmem((2, D * R * TB, H), bf16), vmem((R * TB, H), bf16), vmem((A, H), bf16),
+        vmem((2, D * R * TB, H), bf16), vmem((A, D * R * TB), bf16), vmem((A, H), bf16),
         vmem((2, nt + no, TC, H), bf16), vmem((2, nt + no, TC, H), bf16), vmem((2, TC, H), f32),
         vmem((2, R * TB, H), bf16), vmem((TB, 128), f32), vmem((TB, 128), f32),
         vmem((8, TB), f32), vmem((R, 8, TB), f32), vmem((R, 2 * R, TB), f32),
         vmem((D, R, 2 * R, TB), f32), vmem((D, 2, 2 * R, TB), f32),
         vmem((D, 2 * R, TB), f32), vmem((2 * R, TB), f32), vmem((D, 2 * R, H), f32),
-        vmem((128, TB), f32), vmem((D, TB, 128), f32), vmem((R * TB, A), bf16),
+        vmem((128, TB), f32), vmem((D, TB, 128), f32),
         vmem((2, 2, A, F // 2), f32), vmem((2, 2, A, F // 2), bf16), vmem((2, A, F // 2), bf16),
         vmem((2, HI, A, F // 2), bf16), vmem((2, 2, A, F // 2), bf16),
         vmem((R - 1, TB, A), bf16), vmem((R - 1, TB, A), bf16), vmem((C, TB, A), bf16),
         dma(16),
         dma(R - 1), dma(R - 1), dma(HI), dma(HI), dma(HI), dma(HI),
         dma(D - 1), dma(D - 1), dma(D - 1, R - 1), dma(D - 1, R - 1), dma(R - 1), dma(R - 1),
-        dma(2), dma(2, nt + no), dma(D - 1), dma(D - 1),
+        dma(2), dma(2, nt + no), dma(2, D - 1), dma(2, D - 1),
         dma(R - 1), dma(R - 1), dma(groups), dma(groups), dma(planes), dma(2, planes),
         dma(C - 1), dma(C - 1), dma(planes), dma(planes),
         dma(2), dma(2), dma(2, HI - 1), dma(2, HI - 1), dma(2), dma(2),

time: 68.8 us -> 66.8 us (0.971)
  Pallas kernels: 68 us -> 66 us
    pallas_call x1, Pallas kernels: 65.6 us -> 63.6 us  [on_device(): pl.pallas_call(functools.partial(kernel, dims), out_shape=tuple((vmem(sha...]
where the time goes in v4:
time: 66.8 us; the launch traced here: 66.7 us
  Pallas kernels  66 us (99%)
    pallas_call x1, Pallas kernels, on_device(): pl.pallas_call(functools.partial(kernel, dims), out_shape=tuple((vmem(sha...  63.6 us
    pallas_call x1, Pallas kernels, on_device(): pl.pallas_call(put_out, out_shape=tuple((jax.ShapeDtypeStruct(shape, kind...  2.43 us

profile of v4, /device:TPU:0, one launch (start us, length us, event | category | flops | bytes accessed | tf_op | source)
XLA Modules:
  0.0 66.7 jit_solution(16285139691164496727)
XLA Ops:
  0.6 63.6 %shard_map.197 = (f32[2,512,512]{2,1,0:T(8,128)S(1)}, f32[2,128,512]{2,1,0:T(8,128)S(1)}, f32[2,512]{1,0:T(2,128)S(1)}, f32[2,512,512]{2,1,0:T(8,128)S(1)}, f32[...) custom-call(bf16[128,512]{1,0:T(8,128)(2,1)} %observed_at.1, ...), custom_call_target="tpu_custom_call" | custom-call | tf_op jit(solution)/shard_map/pallas_call | solution.py:642
  64.3 2.4 %shard_map.198 = (f32[2,512,512]{2,1,0:T(8,128)}, f32[2,128,512]{2,1,0:T(8,128)}, f32[2,512]{1,0:T(2,128)}, f32[2,512,512]{2,1,0:T(8,128)}, f32[2,128,512]{2,1,0...) custom-call(f32[2,512,512]{2,1,0:T(8,128)S(1)} %get-tuple-element.16.refs_0_, ...), custom_call_target="tpu_custom_call" | custom-call | tf_op jit(solution)/shard_map/pallas_call | solution.py:654

commit v5 on v4

--- a/solution.py
+++ b/solution.py
@@ -16,6 +16,7 @@
 bf16 = jnp.bfloat16
 pace = 5
 lead = 2
+cuts = 2
 pieces = 2
 
 
@@ -45,6 +46,9 @@
             src_ref=src, dst_ref=dst, send_sem=ssem, recv_sem=rsem,
             device_id=where, device_id_type=pl.DeviceIdType.MESH)
 
+    def bulk(region, ssem, rsem):
+        return copy(region, region, ssem, rsem, row=partner)
+
     pairs = [(next_observed_at, tg_own.at[:, :F]), (next_mean_at, next_mean), (noise_at, noise),
              (tact_at, tact), (tin_at.at[0], tin.at[0]), (tin_at.at[1], tin.at[1]),
              (thead_at, thead), (observed_at, on_own.at[:, :F]), (actions_at, on_own.at[:, F:]),
@@ -93,7 +97,7 @@
         return copy(at, at, oo_s.at[e - 1, o - 1], oo_r.at[e - 1, o - 1], row=(row + o) % R)
 
     def rd_copy(o):
-        return copy(rd_own, rd_all.at[row], rd_s.at[o - 1], rd_r.at[o - 1], row=(row + o) % R)
+        return copy(rd_own, rd_all.at[row], rd_s.at[0], rd_r.at[0], row=(row + o) % R)
 
     for o in range(HI):
         tg_copy(o).start()
@@ -110,14 +114,7 @@
         loads[x].wait()
     for k in range(2):
         a16[2 + k] = tact[k].astype(bf16)
-        w16[2 + k] = tin[k].astype(bf16)
-    for x in (7, 8):
-        loads[x].wait()
-    for e in range(1, D):
-        ox_copy(e).start()
-    for o in range(1, R):
-        on_copy(o).start()
-    on_all[dp, row] = on_own[...]
+    w16[2] = tin[0].astype(bf16)
 
     def rows_of(d, block):
         return pl.ds(pl.multiple_of((d * R + block) * TB, TB), TB)
@@ -193,17 +190,19 @@
         return copy(at, at, xs_s.at[k, e - 1], xs_r.at[k, e - 1], dp=(dp + e) % D)
 
     def vt_copy(o):
-        return copy(vt_all.at[row], vt_all.at[row], vt_s.at[o - 1], vt_r.at[o - 1],
+        return copy(vt_all.at[row], vt_all.at[row], vt_s.at[0], vt_r.at[0],
                     row=(row + o) % R)
 
     def gl_copy(x, a):
         c, d = plane[x]
-        return copy(gl.at[dp, a], gl.at[dp, a], gl_s.at[x], gl_r.at[a, x],
+        at = gl.at[dp * 2 + a]
+        return copy(at, at, gl_s.at[x], gl_r.at[0],
                     col=(col + c) % C, dp=(dp + d) % D)
 
     def vo_copy(x):
         r, d = group[x]
-        return copy(vo_all.at[dp, row], vo_all.at[dp, row], vo_s.at[x], vo_r.at[x],
+        at = vo_all.at[dp * R + row]
+        return copy(at, at, vo_s.at[0], vo_r.at[0],
                     row=(row + r) % R, dp=(dp + d) % D)
 
     lane = lax.broadcasted_iota(jnp.int32, (TC, 128), 1)
@@ -229,7 +228,7 @@
 
         @pl.when(q == no - 1)
         def _():
-            vo_all[dp, row] = vals_o[...].T[:2 * R]
+            vo_all[dp * R + row] = vals_o[...].T[:2 * R]
             for x in range(len(group)):
                 vo_copy(x).start()
         for e in range(1, D):
@@ -244,8 +243,7 @@
 
         @pl.when(i == nt + 2 * pieces - 1)
         def _():
-            for o in range(1, R):
-                vt_copy(o).wait_recv()
+            bulk(vt_all.at[:R - 1], vt_s.at[0], vt_r.at[0]).wait_recv()
             total = vt_all[0]
             for r in range(1, R):
                 total = total + vt_all[r]
@@ -254,7 +252,7 @@
             goal = reward + discount * jnp.minimum(total[:R], total[R:])
             mine = lax.broadcasted_iota(jnp.int32, (R, TB), 0) % 2 == a
             goal = jnp.where(mine, goal, 0.0)
-            gl[dp, a] = jnp.concatenate([goal, goal], axis=0)
+            gl[dp * 2 + a] = jnp.concatenate([goal, goal], axis=0)
             for x in range(len(plane)):
                 gl_copy(x, a).start()
 
@@ -264,6 +262,17 @@
     steps = n + lead + pace * (C - 1) // 2
 
     def aside(s):
+        @pl.when(s == 0)
+        def _():
+            w16[3] = tin[1].astype(bf16)
+            for x in (7, 8):
+                loads[x].wait()
+            for e in range(1, D):
+                ox_copy(e).start()
+            for o in range(1, R):
+                on_copy(o).start()
+            on_all[dp, row] = on_own[...]
+
         @pl.when(s == 1)
         def _():
             for x in range(11, 16):
@@ -274,8 +283,7 @@
 
         @pl.when(s == nt)
         def _():
-            for o in range(1, R):
-                rd_copy(o).wait_recv()
+            bulk(rd_all.at[:R - 1], rd_s.at[0], rd_r.at[0]).wait_recv()
 
         @pl.when(s == nt + 2)
         def _():
@@ -370,11 +378,11 @@
     lax.fori_loop(0, steps, step, 0)
 
     def pu_copy(o):
-        return copy(pu_out.at[o - 1], pu_in.at[o - 1], pu_s.at[o - 1], pu_r.at[o - 1],
+        return copy(pu_out.at[o - 1], pu_in.at[o - 1], pu_s.at[0], pu_r.at[0],
                     row=(row + o) % R)
 
     def pz_copy(c):
-        return copy(pz_all.at[col], pz_all.at[col], pz_s.at[c - 1], pz_r.at[c - 1],
+        return copy(pz_all.at[col], pz_all.at[col], pz_s.at[0], pz_r.at[0],
                     col=(col + c) % C)
 
     last = (((1,), (1,)), ((), ()))
@@ -388,22 +396,24 @@
             pu_out[o - 1] = got.astype(bf16)
             pu_copy(o).start()
 
-    for a in range(2):
-        end = C - 1 if a == 0 else 0
-        for x, (c, d) in enumerate(plane):
-            @pl.when((col + C - c) % C == end)
-            def _():
-                gl_copy(x, a).wait_recv()
-
-    for x in range(len(group)):
-        vo_copy(x).wait_recv()
+    ends = (col == 0) | (col == C - 1)
+
+    @pl.when(ends)
+    def _():
+        bulk(gl.at[:2 * D - 1], gl_s.at[0], gl_r.at[0]).wait_recv()
+
+    @pl.when(jnp.logical_not(ends))
+    def _():
+        bulk(gl, gl_s.at[0], gl_r.at[0]).wait_recv()
+
+    bulk(vo_all.at[:D * R - 1], vo_s.at[0], vo_r.at[0]).wait_recv()
 
     epad[...] = jnp.zeros_like(epad)
     for d in range(D):
-        value = vo_all[d, 0]
+        value = vo_all[d * R]
         for r in range(1, R):
-            value = value + vo_all[d, r]
-        err = value - (gl[d, 0] + gl[d, 1])
+            value = value + vo_all[d * R + r]
+        err = value - (gl[2 * d] + gl[2 * d + 1])
         err_own[d] = err
         epad[:2 * R, :] = 2.0 * err
         columns[d] = epad[...].T
@@ -423,11 +433,11 @@
     chief = 1 % C
 
     def er_copy(c):
-        return copy(err_top, err_top, er_s.at[c - 1], er_r.at[c - 1], col=(col + c) % C)
+        return copy(err_top, err_top, er_s.at[c - 1], er_r.at[0], col=(col + c) % C)
 
     def gh_copy(x):
         c, d = plane[x]
-        return copy(gh.at[dp], gh.at[dp], gh_s.at[x], gh_r.at[x],
+        return copy(gh.at[dp], gh.at[dp], gh_s.at[x], gh_r.at[0],
                     col=(col + c) % C, dp=(dp + d) % D)
 
     slot = lax.broadcasted_iota(jnp.int32, (2 * R, H), 0)
@@ -473,8 +483,8 @@
         for o in range(1, HI):
             gb_copy(k, o).start()
 
+    bulk(pu_in, pu_s.at[0], pu_r.at[0]).wait_recv()
     for o in range(1, R):
-        pu_copy(o).wait_recv()
         push_out[...] += pu_in[o - 1].astype(f32)
     pz_all[col] = push_out[...].astype(bf16)
     for c in range(1, C):
@@ -510,8 +520,7 @@
         gc_all[k, lo] = piece.astype(bf16)
         gc_copy(k).start()
 
-    for c in range(1, C):
-        pz_copy(c).wait_recv()
+    bulk(pz_all.at[:C - 1], pz_s.at[0], pz_r.at[0]).wait_recv()
     push = pz_all[0].astype(f32)
     for c in range(1, C):
         push = push + pz_all[c].astype(f32)
@@ -519,17 +528,19 @@
     flag_column[...] = epad[...].T[:, 0:1]
     push_out[...] = push * flag_column[...]
 
-    for c in range(1, C):
-        @pl.when(col == (chief + c) % C)
-        def _():
-            er_copy(c).wait_recv()
+    @pl.when(col != chief)
+    def _():
+        er_copy(1).wait_recv()
     for k in range(2):
         errs_out[k:k + 1, :] = err_top[pl.ds(k * R + row, 1), :]
 
-    for x, (c, d) in enumerate(plane):
-        @pl.when(col == (chief + c) % C)
-        def _():
-            gh_copy(x).wait_recv()
+    @pl.when(col != chief)
+    def _():
+        bulk(gh, gh_s.at[0], gh_r.at[0]).wait_recv()
+
+    @pl.when(col == chief)
+    def _():
+        bulk(gh.at[:D - 1], gh_s.at[0], gh_r.at[0]).wait_recv()
     whole = gh[0]
     for d in range(1, D):
         whole = whole + gh[d]
@@ -553,8 +564,6 @@
             ftg_copy(o, row).wait_send()
     for o in range(1, R):
         on_copy(o).wait_send()
-        rd_copy(o).wait_send()
-        pu_copy(o).wait_send()
         for e in range(1, D):
             oo_copy(e, o).wait_send()
     for e in range(1, D):
@@ -568,15 +577,14 @@
 
         @pl.when(far == C - 1)
         def _():
-            for o in range(1, R):
-                vt_copy(o).wait_send()
+            bulk(vt_all.at[:R - 1], vt_s.at[0], vt_r.at[0]).wait_send()
             for x in range(len(plane)):
                 gl_copy(x, a).wait_send()
 
-    for x in range(len(group)):
-        vo_copy(x).wait_send()
-    for c in range(1, C):
-        pz_copy(c).wait_send()
+    bulk(vo_all.at[:D * R - 1], vo_s.at[0], vo_r.at[0]).wait_send()
+    bulk(rd_all.at[:R - 1], rd_s.at[0], rd_r.at[0]).wait_send()
+    bulk(pz_all.at[:C - 1], pz_s.at[0], pz_r.at[0]).wait_send()
+    bulk(pu_out, pu_s.at[0], pu_r.at[0]).wait_send()
 
     @pl.when(col == chief)
     def _():
@@ -593,8 +601,17 @@
 
 def put_out(*refs):
     count = len(refs) // 2
-    copies = [pltpu.make_async_copy(refs[x], refs[count + x], refs[-1].at[x])
-              for x in range(count)]
+    pairs = []
+    for x in range(count):
+        if len(refs[x].shape) == 3:
+            rows = refs[x].shape[1] // cuts
+            pairs += [(refs[x].at[k, c * rows:(c + 1) * rows],
+                       refs[count + x].at[k, c * rows:(c + 1) * rows])
+                      for k in range(2) for c in range(cuts)]
+        else:
+            pairs.append((refs[x], refs[count + x]))
+    copies = [pltpu.make_async_copy(src, dst, refs[-1].at[x])
+              for x, (src, dst) in enumerate(pairs)]
     for one in copies:
         one.start()
     for one in copies:
@@ -606,7 +623,7 @@
     R, C, D, TB, F, H, A = dims
     HI, TC = R // 2, TB // pieces
     nt, no = 2 * HI * pieces, 2 * R * pieces
-    planes, groups = C * D - 1, R * D - 1
+    planes = C * D - 1
     dma = lambda *shape: pltpu.SemaphoreType.DMA(shape)
     vmem = pltpu.VMEM
     scratch = [
@@ -621,7 +638,7 @@
         vmem((2, nt + no, TC, H), bf16), vmem((2, nt + no, TC, H), bf16), vmem((2, TC, H), f32),
         vmem((2, R * TB, H), bf16), vmem((TB, 128), f32), vmem((TB, 128), f32),
         vmem((8, TB), f32), vmem((R, 8, TB), f32), vmem((R, 2 * R, TB), f32),
-        vmem((D, R, 2 * R, TB), f32), vmem((D, 2, 2 * R, TB), f32),
+        vmem((D * R, 2 * R, TB), f32), vmem((D * 2, 2 * R, TB), f32),
         vmem((D, 2 * R, TB), f32), vmem((2 * R, TB), f32), vmem((D, 2 * R, H), f32),
         vmem((128, TB), f32), vmem((D, TB, 128), f32),
         vmem((2, 2, A, F // 2), f32), vmem((2, 2, A, F // 2), bf16), vmem((2, A, F // 2), bf16),
@@ -629,12 +646,12 @@
         vmem((R - 1, TB, A), bf16), vmem((R - 1, TB, A), bf16), vmem((C, TB, A), bf16),
         dma(16),
         dma(R - 1), dma(R - 1), dma(HI), dma(HI), dma(HI), dma(HI),
-        dma(D - 1), dma(D - 1), dma(D - 1, R - 1), dma(D - 1, R - 1), dma(R - 1), dma(R - 1),
+        dma(D - 1), dma(D - 1), dma(D - 1, R - 1), dma(D - 1, R - 1), dma(1), dma(1),
         dma(2), dma(2, nt + no), dma(2, D - 1), dma(2, D - 1),
-        dma(R - 1), dma(R - 1), dma(groups), dma(groups), dma(planes), dma(2, planes),
-        dma(C - 1), dma(C - 1), dma(planes), dma(planes),
+        dma(1), dma(1), dma(1), dma(1), dma(planes), dma(1),
+        dma(C - 1), dma(1), dma(planes), dma(1),
         dma(2), dma(2), dma(2, HI - 1), dma(2, HI - 1), dma(2), dma(2),
-        dma(R - 1), dma(R - 1), dma(C - 1), dma(C - 1),
+        dma(1), dma(1), dma(1), dma(1),
     ]
     spec = pl.BlockSpec(memory_space=vmem)
     results = (((2, F, H), f32), ((2, A, F), f32), ((2, H), f32), ((2, F, H), f32),
@@ -656,7 +673,7 @@
         out_shape=tuple(jax.ShapeDtypeStruct(shape, kind) for shape, kind in results),
         in_specs=[spec] * len(results),
         out_specs=(pl.BlockSpec(memory_space=pl.ANY),) * len(results),
-        scratch_shapes=[dma(len(results))],
+        scratch_shapes=[dma(8 * cuts + 4)],
         compiler_params=pltpu.CompilerParams(vmem_limit_bytes=12 * 2 ** 20),
     )(*[pltpu.with_memory_space_constraint(one, vmem) for one in kept])
 

time: 66.8 us -> 66.4 us (level)
  no operation moved by 1% of the time
where the time goes in v5:
time: 66.4 us; the launch traced here: 66.2 us
  Pallas kernels  65.6 us (99%)
    pallas_call x1, Pallas kernels, on_device(): pl.pallas_call(functools.partial(kernel, dims), out_shape=tuple((vmem(sha...  63.1 us
    pallas_call x1, Pallas kernels, on_device(): pl.pallas_call(put_out, out_shape=tuple((jax.ShapeDtypeStruct(shape, kind...  2.51 us

profile of v5, /device:TPU:0, one launch (start us, length us, event | category | flops | bytes accessed | tf_op | source)
XLA Modules:
  0.0 66.2 jit_solution(7561359881186734030)
XLA Ops:
  0.6 63.1 %shard_map.197 = (f32[2,512,512]{2,1,0:T(8,128)S(1)}, f32[2,128,512]{2,1,0:T(8,128)S(1)}, f32[2,512]{1,0:T(2,128)S(1)}, f32[2,512,512]{2,1,0:T(8,128)S(1)}, f32[...) custom-call(bf16[128,512]{1,0:T(8,128)(2,1)} %observed_at.1, ...), custom_call_target="tpu_custom_call" | custom-call | tf_op jit(solution)/shard_map/pallas_call | solution.py:659
  63.7 2.5 %shard_map.198 = (f32[2,512,512]{2,1,0:T(8,128)}, f32[2,128,512]{2,1,0:T(8,128)}, f32[2,512]{1,0:T(2,128)}, f32[2,512,512]{2,1,0:T(8,128)}, f32[2,128,512]{2,1,0...) custom-call(f32[2,512,512]{2,1,0:T(8,128)S(1)} %get-tuple-element.16.refs_0_, ...), custom_call_target="tpu_custom_call" | custom-call | tf_op jit(solution)/shard_map/pallas_call | solution.py:671

commit v6 on v5

--- a/solution.py
+++ b/solution.py
@@ -323,13 +323,9 @@
                 start = (jnp.where(early, D * R + tb, dp * R + ob) * TB
                          + jnp.where(early, tp, op) * TC)
 
-                @pl.when(early)
+                @pl.when(s == 0)
                 def _():
                     prepare_tg(a, i)
-
-                @pl.when((q >= 0) & jnp.logical_not(later(a, far)))
-                def _():
-                    prepare_on(q)
                 mine[a] = jnp.dot(emb[kk, pl.ds(pl.multiple_of(start, TC), TC), :],
                                   w16[jnp.where(early, 2, 0) + kk],
                                   preferred_element_type=f32)
@@ -361,6 +357,14 @@
                 def _():
                     finish_t(a, i, mine[a])
                 forward_tg(a, i, far)
+
+            @pl.when((s > 0) & (i == -1) | live & (i < nt - 1))
+            def _():
+                prepare_tg(a, i + 1)
+
+            @pl.when((i >= nt - 1) & (i < n - 1) & jnp.logical_not(later(a, far)))
+            def _():
+                prepare_on(i + 1 - nt)
 
             @pl.when(live & (i >= nt) & later(a, far))
             def _():

time: 66.4 us -> 66.5 us (level)
  no operation moved by 1% of the time
where the time goes in v6:
time: 66.5 us; the launch traced here: 66.3 us
  Pallas kernels  65.7 us (99%)
    pallas_call x1, Pallas kernels, on_device(): pl.pallas_call(functools.partial(kernel, dims), out_shape=tuple((vmem(sha...  63.2 us
    pallas_call x1, Pallas kernels, on_device(): pl.pallas_call(put_out, out_shape=tuple((jax.ShapeDtypeStruct(shape, kind...  2.51 us

profile of v6, /device:TPU:0, one launch (start us, length us, event | category | flops | bytes accessed | tf_op | source)
XLA Modules:
  0.0 66.3 jit_solution(12216436497623118835)
XLA Ops:
  0.6 63.2 %shard_map.197 = (f32[2,512,512]{2,1,0:T(8,128)S(1)}, f32[2,128,512]{2,1,0:T(8,128)S(1)}, f32[2,512]{1,0:T(2,128)S(1)}, f32[2,512,512]{2,1,0:T(8,128)S(1)}, f32[...) custom-call(bf16[128,512]{1,0:T(8,128)(2,1)} %observed_at.1, ...), custom_call_target="tpu_custom_call" | custom-call | tf_op jit(solution)/shard_map/pallas_call | solution.py:663
  63.8 2.5 %shard_map.198 = (f32[2,512,512]{2,1,0:T(8,128)}, f32[2,128,512]{2,1,0:T(8,128)}, f32[2,512]{1,0:T(2,128)}, f32[2,512,512]{2,1,0:T(8,128)}, f32[2,128,512]{2,1,0...) custom-call(f32[2,512,512]{2,1,0:T(8,128)S(1)} %get-tuple-element.16.refs_0_, ...), custom_call_target="tpu_custom_call" | custom-call | tf_op jit(solution)/shard_map/pallas_call | solution.py:675
